TPU v7x, 256 devices: a whole 4x4x8 slice. The times are simulated.
256 devices in a mesh: gx: 4 (over z_lo), gy: 8 (over z_hi, x), gz: 8 (over y, core).
Axes of the slice: x: 4, y: 4, z: 8 (z_hi: 2, z_lo: 4; z = z_hi * 4 + z_lo), core: 2. Of those that a mesh axis runs over, the one named last changes fastest.
Arguments:
- volume: bfloat16 [32, 8, 128, 1024], P(None, 'gx', 'gy', 'gz'), may hold values from -6 to 6
- w_first: bfloat16 [3, 3, 3, 32, 32], replicated, may hold values from -0.21875 to 0.21875
- w_second: bfloat16 [3, 3, 3, 32, 32], replicated, may hold values from -0.21875 to 0.21875
- v_first: bfloat16 [3, 3, 3, 32, 32], replicated, may hold values from -0.21875 to 0.21875
- v_second: bfloat16 [3, 3, 3, 32, 32], replicated, may hold values from -0.21875 to 0.21875
Outputs:
- jv: bfloat16 [32, 8, 128, 1024], P(None, 'gx', 'gy', 'gz')
- gv_first: float32 [3, 3, 3, 32, 32], replicated
- gv_second: float32 [3, 3, 3, 32, 32], replicated
All inputs are finite; a program needn't handle non-finite values.
Results may differ from a plain program's by a relative error of at most 0.005.
Values may be sent and summed in bfloat16 or wider, within the bound.
A program may use at most 64 MiB of HBM per device.

v0:
```python
import math

import jax
import jax.numpy as jnp
from jax import lax
from jax.sharding import PartitionSpec as P


def padded_2(cells, sides, width):
    for axis, dim in sides:
        count = lax.axis_size(axis)
        ends = count - 1
        head = lax.slice_in_dim(cells, 0, width, axis=dim)
        tail = lax.slice_in_dim(cells, cells.shape[dim] - width, cells.shape[dim], axis=dim)
        cells = jnp.concatenate(
            [
                lax.ppermute(tail, axis, [(i, (i + 1) % count) for i in range(ends)]),
                cells,
                lax.ppermute(head, axis, [((i + 1) % count, i) for i in range(ends)]),
            ],
            axis=dim,
        )
    return cells


def gelu_pair(pre):
    inner = 0.7978845608 * (pre + 0.044715 * pre * pre * pre)
    hyper = jnp.tanh(inner)
    hidden = 0.5 * pre * (1.0 + hyper)
    slope = 0.5 * (1.0 + hyper) + 0.5 * pre * (1.0 - hyper * hyper) * 0.7978845608 * (
        1.0 + 0.134145 * pre * pre
    )
    return (hidden, slope)


def stencil(padded, weight):
    depth = padded.shape[1] - 2
    height = padded.shape[2] - 2
    width = padded.shape[3] - 2
    in_chan = weight.shape[3]
    out_chan = weight.shape[4]
    summed = jnp.zeros((out_chan, depth, height, width), jnp.float32)
    for shift_x in range(3):
        for shift_y in range(3):
            stacked = jnp.concatenate(
                [
                    padded[
                        :,
                        shift_x : shift_x + depth,
                        shift_y : shift_y + height,
                        shift_z : shift_z + width,
                    ]
                    for shift_z in range(3)
                ],
                axis=0,
            )
            matrix = weight[shift_x, shift_y].reshape(3 * in_chan, out_chan)
            summed = summed + jnp.einsum(
                "kxyz,ko->oxyz", stacked, matrix, preferred_element_type=jnp.float32
            )
    return summed


def correlate(padded, target):
    depth = target.shape[1]
    height = target.shape[2]
    width = target.shape[3]
    in_chan = padded.shape[0]
    out_chan = target.shape[0]
    planes = []
    for shift_x in range(3):
        rows_y = []
        for shift_y in range(3):
            stacked = jnp.concatenate(
                [
                    padded[
                        :,
                        shift_x : shift_x + depth,
                        shift_y : shift_y + height,
                        shift_z : shift_z + width,
                    ]
                    for shift_z in range(3)
                ],
                axis=0,
            )
            product = jnp.einsum(
                "kxyz,oxyz->ko", stacked, target, preferred_element_type=jnp.float32
            )
            rows_y.append(product.reshape(3, in_chan, out_chan))
        planes.append(jnp.stack(rows_y))
    return jnp.stack(planes)


def body(volume, w_first, w_second, v_first, v_second):
    channels = volume.shape[0]
    depth = volume.shape[1]
    height = volume.shape[2]
    width = volume.shape[3]
    count_all = float(
        depth * height * width * lax.axis_size("gx") * lax.axis_size("gy") * lax.axis_size("gz")
    )
    factor = math.sqrt(27.0 * channels)
    input_pad = padded_2(volume, (("gx", 1), ("gy", 2), ("gz", 3)), 1)
    pre = stencil(input_pad, w_first)
    hidden_f, slope = gelu_pair(pre)
    hidden = hidden_f.astype(jnp.bfloat16)
    tangent = (slope * stencil(input_pad, v_first)).astype(jnp.bfloat16)
    paired = padded_2(jnp.stack([hidden, tangent]), (("gx", 2), ("gy", 3), ("gz", 4)), 1)
    hidden_pad = paired[0]
    tangent_pad = paired[1]
    jv = (stencil(tangent_pad, w_second) + stencil(hidden_pad, v_second)).astype(jnp.bfloat16)
    local_second = correlate(hidden_pad, jv)
    jv_pad = padded_2(jv, (("gx", 1), ("gy", 2), ("gz", 3)), 1)
    flipped = jnp.transpose(jnp.flip(w_second, (0, 1, 2)), (0, 1, 2, 4, 3))
    back = (slope * stencil(jv_pad, flipped)).astype(jnp.bfloat16)
    local_first = correlate(input_pad, back)
    summed_first, summed_second = lax.psum((local_first, local_second), ("gx", "gy", "gz"))
    gv_first = factor * (summed_first / count_all + 0.1 * v_first.astype(jnp.float32))
    gv_second = factor * (summed_second / count_all + 0.1 * v_second.astype(jnp.float32))
    return (jv, gv_first, gv_second)


def solution(mesh):
    in_specs = (P(None, "gx", "gy", "gz"), P(), P(), P(), P())
    out_specs = (P(None, "gx", "gy", "gz"), P(), P())
    return jax.shard_map(body, mesh=mesh, in_specs=in_specs, out_specs=out_specs, check_vma=False)
```

profile of v0, /device:TPU:1, one launch (start us, length us, event | category | flops | bytes accessed | tf_op | source)
XLA Modules:
  0.0 442.0 jit_solution(16340484945520998631)
XLA Ops:
  8.4 1.3 collective-permute-start.1
  9.7 5.0 %collective-permute-start = (bf16[32,1,16,128]{3,0,2,1:T(8,128)(2,1)S(1)}, bf16[32,1,16,128]{3,0,2,1:T(8,128)(2,1)S(1)}, u32[]{:S(2)}, u32[]{:S(2)}) collective-permute-start(bf16[32,1,16,128]{3,0,2,1:T(8,128)(2,1)S(1)} %get-tuple-element.141), channel_id=1, source_target_pairs={{0,64},{64,128},{128,192},{1,65},{65,129},{129,193},{2,66},{66,130... | collective-permute-start | bytes 393224 | tf_op jit(solution)/shard_map/ppermute | solution.py:17
  14.7 1.5 fusion.203
  16.8 3.1 collective-permute-start.2
  19.9 1.3 collective-permute-start.3
  21.9 2.7 collective-permute-done.3
  26.5 5.1 %collective-permute-start.5 = (bf16[32,4,18,1]{0,1,3,2:T(4,128)(2,1)S(1)}, bf16[32,4,18,1]{0,1,3,2:T(4,128)(2,1)}, u32[]{:S(2)}, u32[]{:S(2)}) collective-permute-start(bf16[32,4,18,1]{0,1,3,2:T(4,128)(2,1)S(1)} %copy.139), channel_id=1, source_target_pairs={{1,0},{2,1},{3,2},{4,3},{5,4},{6,5},{7,6},{9,8},{10,9},{11,10},{12... | collective-permute-start | bytes 13832 | tf_op jit(solution)/shard_map/ppermute | solution.py:19
  31.6 3.1 collective-permute-start.4
  47.4 4.1 collective-permute-start.6
  51.5 1.3 collective-permute-start.7
  53.5 3.8 collective-permute-done.6
  57.3 4.2 collective-permute-done.7
  61.6 3.1 collective-permute-start.8
  66.7 7.5 %collective-permute-done.9 = bf16[2,32,4,1,128]{4,1,3,2,0:T(8,128)(2,1)S(1)} collective-permute-done((bf16[2,32,4,1,128]{4,1,3,2,0:T(8,128)(2,1)S(1)}, bf16[2,32,4,1,128]{4,1,3,2,0:T(8,128)(2,1)S(1)}, u32[]{:S(2)}, u32[]{:S(2)}) %collective-permute-start.9) | collective-permute-done | bytes 65568 | tf_op jit(solution)/shard_map/ppermute | solution.py:19
  75.7 1.5 copy.162
  78.2 3.5 collective-permute-start.11
  81.6 3.3 collective-permute-start.10
  84.9 1.6 fusion.201
  92.7 1.7 copy.165
  94.4 3.8 pad_maximum_fusion
  113.0 2.6 collective-permute-start.12
  115.6 1.3 collective-permute-start.13
  117.4 1.3 collective-permute-done.12
  118.7 4.3 collective-permute-done.13
  123.0 9.6 %collective-permute-start.14 = (bf16[32,4,1,128]{3,0,2,1:T(8,128)(2,1)S(1)}, bf16[32,4,1,128]{3,0,2,1:T(8,128)(2,1)S(1)}, u32[]{:S(2)}, u32[]{:S(2)}) collective-permute-start(bf16[32,4,1,128]{3,0,2,1:T(8,128)(2,1)S(1)} %get-tuple-element.130), channel_id=1, source_target_pairs={{0,8},{8,16},{16,24},{24,32},{32,40},{40,48},{48,56},{1,9},{9,17},... | collective-permute-start | bytes 98312 | tf_op jit(solution)/shard_map/ppermute | solution.py:17
  132.6 1.5 collective-permute-start.15
  135.1 2.4 collective-permute-done.15
  139.0 3.5 collective-permute-start.17
  142.5 2.8 collective-permute-start.16
  147.5 1.4 maximum_maximum_fusion.1
  167.2 264.3 %all-reduce.3.cloned.1.call-done = (f32[3,3,3,32,32]{3,2,4,1,0:T(4,128)}, f32[3,3,3,32,32]{3,2,4,1,0:T(4,128)}) async-done(((f32[3,3,3,32,32]{3,2,4,1,0:T(4,128)}, f32[3,3,3,32,32]{3,2,4,1,0:T(4,128)}), (f32[3,3,3,32,32]{3,2,4,1,0:T(4,128)}, f32[3,3,3,32,32]{3,2,4,1,0:T(4,128)})) %all-reduce.3.cloned.1.call-update) | async-done | bytes 221200 | tf_op jit(solution)/shard_map/psum | solution.py:117
  431.5 1.4 add_multiply_fusion.1
  (385 shorter events, 67.2 us)
Async XLA Ops:
  7.2 14.1 %copy-start.6 = (bf16[3,3,3,32,32]{4,3,2,1,0:T(8,128)(2,1)S(1)}, bf16[3,3,3,32,32]{4,3,2,1,0:T(8,128)(2,1)}, u32[]{:S(2)}) copy-start(bf16[3,3,3,32,32]{4,3,2,1,0:T(8,128)(2,1)} %param.8) | copy-start | bytes 165892
  7.2 424.4 %all-reduce.3.cloned.1.call-start = ((), (), s32[]{:S(2)}) async-start(), calls=%async_computation | async-start | bytes 2359296 | tf_op jit(solution)/shard_map/psum | solution.py:117
  8.3 38.1 %copy-start.3 = (bf16[32,2,16,128]{3,0,2,1:T(8,128)(2,1)}, bf16[32,2,16,128]{3,0,2,1:T(8,128)(2,1)S(1)}, u32[]{:S(2)}) copy-start(bf16[32,2,16,128]{3,0,2,1:T(8,128)(2,1)S(1)} %copy.134) | copy-start | bytes 786436
  8.4 8.4 %collective-permute-start.1 = (bf16[32,1,16,128]{3,0,2,1:T(8,128)(2,1)S(1)}, bf16[32,1,16,128]{3,0,2,1:T(8,128)(2,1)S(1)}, u32[]{:S(2)}, u32[]{:S(2)}) collective-permute-start(bf16[32,1,16,128]{3,0,2,1:T(8,128)(2,1)S(1)} %get-tuple-element.140), channel_id=1, source_target_pairs={{64,0},{128,64},{192,128},{65,1},{129,65},{193,129},{66,2},{130,66... | collective-permute-start | bytes 393224 | tf_op jit(solution)/shard_map/ppermute | solution.py:19
  9.7 6.9 %collective-permute-start = (bf16[32,1,16,128]{3,0,2,1:T(8,128)(2,1)S(1)}, bf16[32,1,16,128]{3,0,2,1:T(8,128)(2,1)S(1)}, u32[]{:S(2)}, u32[]{:S(2)}) collective-permute-start(bf16[32,1,16,128]{3,0,2,1:T(8,128)(2,1)S(1)} %get-tuple-element.141), channel_id=1, source_target_pairs={{0,64},{64,128},{128,192},{1,65},{65,129},{129,193},{2,66},{66,130... | collective-permute-start | bytes 393224 | tf_op jit(solution)/shard_map/ppermute | solution.py:17
  16.6 27.4 %copy-start.61 = (bf16[32,1,16,128]{3,0,2,1:T(8,128)(2,1)}, bf16[32,1,16,128]{3,0,2,1:T(8,128)(2,1)S(1)}, u32[]{:S(2)}) copy-start(bf16[32,1,16,128]{3,0,2,1:T(8,128)(2,1)S(1)} %collective-permute-done) | copy-start | bytes 393220
  16.8 29.7 %copy-start.59 = (bf16[32,1,16,128]{3,0,2,1:T(8,128)(2,1)}, bf16[32,1,16,128]{3,0,2,1:T(8,128)(2,1)S(1)}, u32[]{:S(2)}) copy-start(bf16[32,1,16,128]{3,0,2,1:T(8,128)(2,1)S(1)} %collective-permute-done.1) | copy-start | bytes 393220
  16.8 5.1 %collective-permute-start.2 = (bf16[32,4,1,128]{3,0,2,1:T(8,128)(2,1)S(1)}, bf16[32,4,1,128]{3,0,2,1:T(8,128)(2,1)S(1)}, u32[]{:S(2)}, u32[]{:S(2)}) collective-permute-start(bf16[32,4,1,128]{3,0,2,1:T(8,128)(2,1)S(1)} %get-tuple-element.136), channel_id=1, source_target_pairs={{0,8},{8,16},{16,24},{24,32},{32,40},{40,48},{48,56},{1,9},{9,17},... | collective-permute-start | bytes 98312 | tf_op jit(solution)/shard_map/ppermute | solution.py:17
  19.9 4.7 %collective-permute-start.3 = (bf16[32,4,1,128]{3,0,2,1:T(8,128)(2,1)S(1)}, bf16[32,4,1,128]{3,0,2,1:T(8,128)(2,1)S(1)}, u32[]{:S(2)}, u32[]{:S(2)}) collective-permute-start(bf16[32,4,1,128]{3,0,2,1:T(8,128)(2,1)S(1)} %get-tuple-element.137), channel_id=1, source_target_pairs={{8,0},{16,8},{24,16},{32,24},{40,32},{48,40},{56,48},{9,1},{17,9},... | collective-permute-start | bytes 98312 | tf_op jit(solution)/shard_map/ppermute | solution.py:19
  26.5 9.8 %collective-permute-start.5 = (bf16[32,4,18,1]{0,1,3,2:T(4,128)(2,1)S(1)}, bf16[32,4,18,1]{0,1,3,2:T(4,128)(2,1)}, u32[]{:S(2)}, u32[]{:S(2)}) collective-permute-start(bf16[32,4,18,1]{0,1,3,2:T(4,128)(2,1)S(1)} %copy.139), channel_id=1, source_target_pairs={{1,0},{2,1},{3,2},{4,3},{5,4},{6,5},{7,6},{9,8},{10,9},{11,10},{12... | collective-permute-start | bytes 13832 | tf_op jit(solution)/shard_map/ppermute | solution.py:19
  31.6 4.2 collective-permute-start.4
  34.9 10.9 %copy-start.23 = (bf16[32,2,16,128]{3,0,2,1:T(8,128)(2,1)}, bf16[32,2,16,128]{3,0,2,1:T(8,128)(2,1)S(1)}, u32[]{:S(2)}) copy-start(bf16[32,2,16,128]{3,0,2,1:T(8,128)(2,1)S(1)} %get-tuple-element.124) | copy-start | bytes 786436
  47.4 9.9 %collective-permute-start.6 = (bf16[2,32,1,16,128]{4,1,3,2,0:T(8,128)(2,1)S(1)}, bf16[2,32,1,16,128]{4,1,3,2,0:T(8,128)(2,1)S(1)}, u32[]{:S(2)}, u32[]{:S(2)}) collective-permute-start(bf16[2,32,1,16,128]{4,1,3,2,0:T(8,128)(2,1)S(1)} %get-tuple-element.132), channel_id=1, source_target_pairs={{0,64},{64,128},{128,192},{1,65},{65,129},{129,193},{2,66},{66,130... | collective-permute-start | bytes 786440 | tf_op jit(solution)/shard_map/ppermute | solution.py:17
  51.5 10.1 %collective-permute-start.7 = (bf16[2,32,1,16,128]{4,1,3,2,0:T(8,128)(2,1)S(1)}, bf16[2,32,1,16,128]{4,1,3,2,0:T(8,128)(2,1)S(1)}, u32[]{:S(2)}, u32[]{:S(2)}) collective-permute-start(bf16[2,32,1,16,128]{4,1,3,2,0:T(8,128)(2,1)S(1)} %get-tuple-element.133), channel_id=1, source_target_pairs={{64,0},{128,64},{192,128},{65,1},{129,65},{193,129},{66,2},{130,66... | collective-permute-start | bytes 786440 | tf_op jit(solution)/shard_map/ppermute | solution.py:19
  57.3 17.0 %copy-start = (bf16[2,32,1,16,128]{4,1,3,2,0:T(8,128)(2,1)}, bf16[2,32,1,16,128]{4,1,3,2,0:T(8,128)(2,1)S(1)}, u32[]{:S(2)}) copy-start(bf16[2,32,1,16,128]{4,1,3,2,0:T(8,128)(2,1)S(1)} %collective-permute-done.6) | copy-start | bytes 786436
  61.5 12.7 %copy-start.1 = (bf16[2,32,1,16,128]{4,1,3,2,0:T(8,128)(2,1)}, bf16[2,32,1,16,128]{4,1,3,2,0:T(8,128)(2,1)S(1)}, u32[]{:S(2)}) copy-start(bf16[2,32,1,16,128]{4,1,3,2,0:T(8,128)(2,1)S(1)} %collective-permute-done.7) | copy-start | bytes 786436
  61.6 5.2 %collective-permute-start.8 = (bf16[2,32,4,1,128]{4,1,3,2,0:T(8,128)(2,1)S(1)}, bf16[2,32,4,1,128]{4,1,3,2,0:T(8,128)(2,1)S(1)}, u32[]{:S(2)}, u32[]{:S(2)}) collective-permute-start(bf16[2,32,4,1,128]{4,1,3,2,0:T(8,128)(2,1)S(1)} %get-tuple-element.108), channel_id=1, source_target_pairs={{0,8},{8,16},{16,24},{24,32},{32,40},{40,48},{48,56},{1,9},{9,17},... | collective-permute-start | bytes 196616 | tf_op jit(solution)/shard_map/ppermute | solution.py:17
  64.7 9.5 %collective-permute-start.9 = (bf16[2,32,4,1,128]{4,1,3,2,0:T(8,128)(2,1)S(1)}, bf16[2,32,4,1,128]{4,1,3,2,0:T(8,128)(2,1)S(1)}, u32[]{:S(2)}, u32[]{:S(2)}) collective-permute-start(bf16[2,32,4,1,128]{4,1,3,2,0:T(8,128)(2,1)S(1)} %get-tuple-element.109), channel_id=1, source_target_pairs={{8,0},{16,8},{24,16},{32,24},{40,32},{48,40},{56,48},{9,1},{17,9},... | collective-permute-start | bytes 196616 | tf_op jit(solution)/shard_map/ppermute | solution.py:19
  77.2 10.3 %copy-start.69 = (bf16[1,1,3,32,32]{3,4,2,1,0:T(8,128)(2,1)S(1)}, bf16[1,1,3,32,32]{3,4,2,1,0:T(8,128)(2,1)}, u32[]{:S(2)}) copy-start(bf16[1,1,3,32,32]{3,4,2,1,0:T(8,128)(2,1)} %get-tuple-element.145) | copy-start | bytes 18436
  77.2 11.0 %copy-start.68 = (bf16[1,1,3,32,32]{3,4,2,1,0:T(8,128)(2,1)S(1)}, bf16[1,1,3,32,32]{3,4,2,1,0:T(8,128)(2,1)}, u32[]{:S(2)}) copy-start(bf16[1,1,3,32,32]{3,4,2,1,0:T(8,128)(2,1)} %get-tuple-element.146) | copy-start | bytes 18436
  77.2 11.7 %copy-start.67 = (bf16[1,1,3,32,32]{3,4,2,1,0:T(8,128)(2,1)S(1)}, bf16[1,1,3,32,32]{3,4,2,1,0:T(8,128)(2,1)}, u32[]{:S(2)}) copy-start(bf16[1,1,3,32,32]{3,4,2,1,0:T(8,128)(2,1)} %get-tuple-element.147) | copy-start | bytes 18436
  77.2 12.4 %copy-start.66 = (bf16[1,1,3,32,32]{3,4,2,1,0:T(8,128)(2,1)S(1)}, bf16[1,1,3,32,32]{3,4,2,1,0:T(8,128)(2,1)}, u32[]{:S(2)}) copy-start(bf16[1,1,3,32,32]{3,4,2,1,0:T(8,128)(2,1)} %get-tuple-element.148) | copy-start | bytes 18436
  77.2 13.1 %copy-start.65 = (bf16[1,1,3,32,32]{3,4,2,1,0:T(8,128)(2,1)S(1)}, bf16[1,1,3,32,32]{3,4,2,1,0:T(8,128)(2,1)}, u32[]{:S(2)}) copy-start(bf16[1,1,3,32,32]{3,4,2,1,0:T(8,128)(2,1)} %get-tuple-element.149) | copy-start | bytes 18436
  77.3 13.8 %copy-start.64 = (bf16[1,1,3,32,32]{3,4,2,1,0:T(8,128)(2,1)S(1)}, bf16[1,1,3,32,32]{3,4,2,1,0:T(8,128)(2,1)}, u32[]{:S(2)}) copy-start(bf16[1,1,3,32,32]{3,4,2,1,0:T(8,128)(2,1)} %get-tuple-element.150) | copy-start | bytes 18436
  78.2 14.5 %collective-permute-start.11 = (bf16[2,32,4,18,1]{1,2,4,3,0:T(4,128)(2,1)S(1)}, bf16[2,32,4,18,1]{1,2,4,3,0:T(4,128)(2,1)}, u32[]{:S(2)}, u32[]{:S(2)}) collective-permute-start(bf16[2,32,4,18,1]{1,2,4,3,0:T(4,128)(2,1)S(1)} %copy.163), channel_id=1, source_target_pairs={{1,0},{2,1},{3,2},{4,3},{5,4},{6,5},{7,6},{9,8},{10,9},{11,10},{12... | collective-permute-start | bytes 27656 | tf_op jit(solution)/shard_map/ppermute | solution.py:19
  81.6 10.1 %collective-permute-start.10 = (bf16[2,32,4,18,1]{1,2,4,3,0:T(4,128)(2,1)}, bf16[2,32,4,18,1]{1,2,4,3,0:T(4,128)(2,1)S(1)}, u32[]{:S(2)}, u32[]{:S(2)}) collective-permute-start(bf16[2,32,4,18,1]{1,2,4,3,0:T(4,128)(2,1)} %copy.162), channel_id=1, source_target_pairs={{0,1},{1,2},{2,3},{3,4},{4,5},{5,6},{6,7},{8,9},{9,10},{10,11},{11... | collective-permute-start | bytes 27656 | tf_op jit(solution)/shard_map/ppermute | solution.py:17
  113.0 5.7 %collective-permute-start.12 = (bf16[32,1,16,128]{3,0,2,1:T(8,128)(2,1)S(1)}, bf16[32,1,16,128]{3,0,2,1:T(8,128)(2,1)S(1)}, u32[]{:S(2)}, u32[]{:S(2)}) collective-permute-start(bf16[32,1,16,128]{3,0,2,1:T(8,128)(2,1)S(1)} %get-tuple-element.138), channel_id=1, source_target_pairs={{0,64},{64,128},{128,192},{1,65},{65,129},{129,193},{2,66},{66,130... | collective-permute-start | bytes 393224 | tf_op jit(solution)/shard_map/ppermute | solution.py:17
  115.6 7.3 %collective-permute-start.13 = (bf16[32,1,16,128]{3,0,2,1:T(8,128)(2,1)S(1)}, bf16[32,1,16,128]{3,0,2,1:T(8,128)(2,1)S(1)}, u32[]{:S(2)}, u32[]{:S(2)}) collective-permute-start(bf16[32,1,16,128]{3,0,2,1:T(8,128)(2,1)S(1)} %get-tuple-element.139), channel_id=1, source_target_pairs={{64,0},{128,64},{192,128},{65,1},{129,65},{193,129},{66,2},{130,66... | collective-permute-start | bytes 393224 | tf_op jit(solution)/shard_map/ppermute | solution.py:19
  123.0 12.2 %collective-permute-start.14 = (bf16[32,4,1,128]{3,0,2,1:T(8,128)(2,1)S(1)}, bf16[32,4,1,128]{3,0,2,1:T(8,128)(2,1)S(1)}, u32[]{:S(2)}, u32[]{:S(2)}) collective-permute-start(bf16[32,4,1,128]{3,0,2,1:T(8,128)(2,1)S(1)} %get-tuple-element.130), channel_id=1, source_target_pairs={{0,8},{8,16},{16,24},{24,32},{32,40},{40,48},{48,56},{1,9},{9,17},... | collective-permute-start | bytes 98312 | tf_op jit(solution)/shard_map/ppermute | solution.py:17
  132.6 5.0 %collective-permute-start.15 = (bf16[32,4,1,128]{3,0,2,1:T(8,128)(2,1)S(1)}, bf16[32,4,1,128]{3,0,2,1:T(8,128)(2,1)S(1)}, u32[]{:S(2)}, u32[]{:S(2)}) collective-permute-start(bf16[32,4,1,128]{3,0,2,1:T(8,128)(2,1)S(1)} %get-tuple-element.131), channel_id=1, source_target_pairs={{8,0},{16,8},{24,16},{32,24},{40,32},{48,40},{56,48},{9,1},{17,9},... | collective-permute-start | bytes 98312 | tf_op jit(solution)/shard_map/ppermute | solution.py:19
  139.0 8.0 %collective-permute-start.17 = (bf16[32,4,18,1]{0,1,3,2:T(4,128)(2,1)S(1)}, bf16[32,4,18,1]{0,1,3,2:T(4,128)(2,1)S(1)}, u32[]{:S(2)}, u32[]{:S(2)}) collective-permute-start(bf16[32,4,18,1]{0,1,3,2:T(4,128)(2,1)S(1)} %copy.186), channel_id=1, source_target_pairs={{1,0},{2,1},{3,2},{4,3},{5,4},{6,5},{7,6},{9,8},{10,9},{11,10},{12... | collective-permute-start | bytes 13832 | tf_op jit(solution)/shard_map/ppermute | solution.py:19
  142.5 3.9 collective-permute-start.16
  (94 other events, 239.1 us)
Sparse Core Ops, SparseCore 0:
  166.1 265.4 all-reduce.2
where the time goes:
time: 446 us; the launch traced here: 442 us
  waiting for transfers between devices  292 us (65%)
  starting transfers between devices  56.9 us (13%)
  local copies, waits for them, and re-layouts  47.2 us (11%)
  matrix products  19.3 us (4%)
  between operations  15.7 us (4%)
  other arithmetic  10.9 us (2%)
    psum x1, waiting for transfers between devices, body(): lax.psum((local_first, local_second), ('gx', 'gy', 'gz'))  264 us
    ppermute x9, starting transfers between devices, padded_2(): lax.ppermute(tail, axis, [(i, (i + 1) % count) for i in range(ends)])  36.8 us
    ppermute x9, waiting for transfers between devices, padded_2(): lax.ppermute(head, axis, [((i + 1) % count, i) for i in range(ends)])  21.2 us
    ppermute x9, starting transfers between devices, padded_2(): lax.ppermute(head, axis, [((i + 1) % count, i) for i in range(ends)])  20 us
    unnamed x222, local copies, waits for them, and re-layouts  16.6 us
    dot_general x45, matrix products, stencil(): jnp.einsum('kxyz,ko->oxyz', stacked, matrix, preferred_element_type=jnp.f...  12.7 us
  transfers between devices with their start and end apart: 19, of which 10 were waited for; matrix products, arithmetic and copies ran while one was open for 4% of the time, Pallas kernels for 0%

commit v1 on v0

--- a/solution.py
+++ b/solution.py
@@ -1,9 +1,143 @@
+import functools
 import math
 
 import jax
 import jax.numpy as jnp
 from jax import lax
+from jax.experimental import pallas as pl
+from jax.experimental.pallas import tpu as pltpu
 from jax.sharding import PartitionSpec as P
+
+MESH = pl.DeviceIdType.MESH
+
+
+def reduce_kernel(nx, ny, nz, x_ref, o_ref, recv1, rows, recv2, gath, chunk, s1, r1, s2, r2, s3, r3, s4, r4):
+    ix, iy, iz = lax.axis_index("gx"), lax.axis_index("gy"), lax.axis_index("gz")
+    plane = nx * ny
+    me = iy * nx + ix
+
+    def z_peer(d):
+        return {"gx": ix, "gy": iy, "gz": lax.rem(iz + d, nz)}
+
+    def p_peer(d):
+        q = lax.rem(me + d, plane)
+        return q, {"gx": lax.rem(q, nx), "gy": q // nx, "gz": iz}
+
+    barrier = pltpu.get_barrier_semaphore()
+    for d in range(1, nz):
+        pl.semaphore_signal(barrier, inc=1, device_id=z_peer(d), device_id_type=MESH)
+
+    def greet(d, _):
+        pl.semaphore_signal(barrier, inc=1, device_id=p_peer(d)[1], device_id_type=MESH)
+        return 0
+
+    lax.fori_loop(1, plane, greet, 0)
+    pl.semaphore_wait(barrier, nz - 1 + plane - 1)
+
+    def send1(d):
+        peer = z_peer(d)
+        return pltpu.make_async_remote_copy(
+            x_ref.at[peer["gz"]], recv1.at[d - 1], s1.at[d - 1], r1.at[d - 1], device_id=peer, device_id_type=MESH
+        )
+
+    for d in range(1, nz):
+        send1(d).start()
+    total = x_ref[iz]
+    for d in range(1, nz):
+        send1(d).wait_recv()
+        total = total + recv1[d - 1]
+    for f in range(2):
+        for q in range(plane):
+            rows[q, f : f + 1, :] = total[f, q // 8, q % 8 : q % 8 + 1, :]
+
+    def send2(d):
+        q, peer = p_peer(d)
+        return pltpu.make_async_remote_copy(
+            rows.at[q], recv2.at[d - 1], s2.at[d - 1], r2.at[d - 1], device_id=peer, device_id_type=MESH
+        )
+
+    def send3(d):
+        q, peer = p_peer(d)
+        return pltpu.make_async_remote_copy(
+            gath.at[me], gath.at[me], s3.at[d - 1], r3.at[d - 1], device_id=peer, device_id_type=MESH
+        )
+
+    def start2(d, _):
+        send2(d).start()
+        return 0
+
+    def take2(d, acc):
+        send2(d).wait_recv()
+        return acc + recv2[d - 1]
+
+    def start3(d, _):
+        send3(d).start()
+        return 0
+
+    def take3(d, _):
+        send3(d).wait_recv()
+        return 0
+
+    lax.fori_loop(1, plane, start2, 0)
+    gath[me] = lax.fori_loop(1, plane, take2, rows[me])
+    lax.fori_loop(1, plane, start3, 0)
+    lax.fori_loop(1, plane, take3, 0)
+    for f in range(2):
+        for q in range(plane):
+            chunk[f, q // 8, q % 8 : q % 8 + 1, :] = gath[q, f : f + 1, :]
+
+    def send4(d):
+        return pltpu.make_async_remote_copy(
+            chunk, o_ref.at[iz], s4.at[d - 1], r4.at[d - 1], device_id=z_peer(d), device_id_type=MESH
+        )
+
+    for d in range(1, nz):
+        send4(d).start()
+    o_ref[iz] = chunk[...]
+    for d in range(1, nz):
+        send4(d).wait_recv()
+    for d in range(1, nz):
+        send1(d).wait_send()
+        send4(d).wait_send()
+
+    def drain(d, _):
+        send2(d).wait_send()
+        send3(d).wait_send()
+        return 0
+
+    lax.fori_loop(1, plane, drain, 0)
+
+
+def all_sums(first, second):
+    nx, ny, nz = lax.axis_size("gx"), lax.axis_size("gy"), lax.axis_size("gz")
+    plane = nx * ny
+    tiles = plane // 8
+    size = first.size
+    whole = nz * plane * 128
+    flat = jnp.stack([first.reshape(-1), second.reshape(-1)])
+    flat = jnp.pad(flat, ((0, 0), (0, whole - size))).reshape(2, nz, tiles, 8, 128)
+    flat = jnp.transpose(flat, (1, 0, 2, 3, 4))
+    dma = pltpu.SemaphoreType.DMA
+    out = pl.pallas_call(
+        functools.partial(reduce_kernel, nx, ny, nz),
+        out_shape=jax.ShapeDtypeStruct((nz, 2, tiles, 8, 128), jnp.float32),
+        in_specs=[pl.BlockSpec(memory_space=pltpu.VMEM)],
+        out_specs=pl.BlockSpec(memory_space=pltpu.VMEM),
+        scratch_shapes=[
+            pltpu.VMEM((nz - 1, 2, tiles, 8, 128), jnp.float32),
+            pltpu.VMEM((plane, 2, 128), jnp.float32),
+            pltpu.VMEM((plane - 1, 2, 128), jnp.float32),
+            pltpu.VMEM((plane, 2, 128), jnp.float32),
+            pltpu.VMEM((2, tiles, 8, 128), jnp.float32),
+            dma((nz - 1,)), dma((nz - 1,)),
+            dma((plane - 1,)), dma((plane - 1,)),
+            dma((plane - 1,)), dma((plane - 1,)),
+            dma((nz - 1,)), dma((nz - 1,)),
+        ],
+        compiler_params=pltpu.CompilerParams(collective_id=0, has_side_effects=True),
+    )(flat)
+    out = jnp.transpose(out, (1, 0, 2, 3, 4)).reshape(2, whole)[:, :size]
+    return out[0].reshape(first.shape), out[1].reshape(second.shape)
 
 
 def padded_2(cells, sides, width):
@@ -114,7 +248,7 @@
     flipped = jnp.transpose(jnp.flip(w_second, (0, 1, 2)), (0, 1, 2, 4, 3))
     back = (slope * stencil(jv_pad, flipped)).astype(jnp.bfloat16)
     local_first = correlate(input_pad, back)
-    summed_first, summed_second = lax.psum((local_first, local_second), ("gx", "gy", "gz"))
+    summed_first, summed_second = all_sums(local_first, local_second)
     gv_first = factor * (summed_first / count_all + 0.1 * v_first.astype(jnp.float32))
     gv_second = factor * (summed_second / count_all + 0.1 * v_second.astype(jnp.float32))
     return (jv, gv_first, gv_second)

time: 446 us -> 208 us (0.47)
  waiting for transfers between devices: 292 us -> 11.4 us
  Pallas kernels: 0 us -> 54.3 us
  between operations: 15.7 us -> 2.5 us
    psum x1 -> x0, waiting for transfers between devices: 264 us -> none  [body(): lax.psum((local_first, local_second), ('gx', 'gy', 'gz'))]
    pallas_call x0 -> x1, Pallas kernels: none -> 54.3 us  [all_sums(): pl.pallas_call(functools.partial(reduce_kernel, nx, ny, nz), out_shape=ja...]
    ppermute x9, waiting for transfers between devices: 21.2 us -> 7.79 us  [padded_2(): lax.ppermute(head, axis, [((i + 1) % count, i) for i in range(ends)])]
    ppermute x9, starting transfers between devices: 20 us -> 13.6 us  [padded_2(): lax.ppermute(head, axis, [((i + 1) % count, i) for i in range(ends)])]
    ppermute x9, starting transfers between devices: 36.8 us -> 42.6 us  [padded_2(): lax.ppermute(tail, axis, [(i, (i + 1) % count) for i in range(ends)])]
    unnamed x222 -> x230, local copies, waits for them, and re-layouts: 16.6 us -> 15 us
  transfers between devices with their start and end apart: 19 -> 18, of which waited for: 10 -> 7; matrix products, arithmetic and copies ran while one was open for 4% -> 10% of each run, Pallas kernels for 0% -> 0%
where the time goes in v1:
time: 208 us; the launch traced here: 205 us
  starting transfers between devices  56.2 us (27%)
  Pallas kernels  54.3 us (26%)
  local copies, waits for them, and re-layouts  49.2 us (24%)
  matrix products  21 us (10%)
  waiting for transfers between devices  11.4 us (5%)
  other arithmetic  10.9 us (5%)
  between operations  2.5 us (1%)
    pallas_call x1, Pallas kernels, all_sums(): pl.pallas_call(functools.partial(reduce_kernel, nx, ny, nz), out_shape=ja...  54.3 us
    ppermute x9, starting transfers between devices, padded_2(): lax.ppermute(tail, axis, [(i, (i + 1) % count) for i in range(ends)])  42.6 us
    unnamed x230, local copies, waits for them, and re-layouts  15 us
    ppermute x9, starting transfers between devices, padded_2(): lax.ppermute(head, axis, [((i + 1) % count, i) for i in range(ends)])  13.6 us
    dot_general x45, matrix products, stencil(): jnp.einsum('kxyz,ko->oxyz', stacked, matrix, preferred_element_type=jnp.f...  12.7 us
    dot_general x18, matrix products, correlate(): jnp.einsum('kxyz,oxyz->ko', stacked, target, preferred_element_type=jnp.f...  8.27 us
    ppermute x9, waiting for transfers between devices, padded_2(): lax.ppermute(head, axis, [((i + 1) % count, i) for i in range(ends)])  7.79 us
    concatenate x8, other arithmetic, padded_2(): jnp.concatenate([lax.ppermute(tail, axis, [(i, (i + 1) % count) for i in...  7.43 us
  transfers between devices with their start and end apart: 18, of which 7 were waited for; matrix products, arithmetic and copies ran while one was open for 10% of the time, Pallas kernels for 0%

profile of v1, /device:TPU:1, one launch (start us, length us, event | category | flops | bytes accessed | tf_op | source)
XLA Modules:
  0.0 205.5 jit_solution(3889521540885421000)
XLA Ops:
  1.8 4.4 %collective-permute-start = (bf16[32,1,16,128]{3,0,2,1:T(8,128)(2,1)S(1)}, bf16[32,1,16,128]{3,0,2,1:T(8,128)(2,1)S(1)}, u32[]{:S(2)}, u32[]{:S(2)}) collective-permute-start(bf16[32,1,16,128]{3,0,2,1:T(8,128)(2,1)S(1)} %get-tuple-element.141), channel_id=1, source_target_pairs={{0,64},{64,128},{128,192},{1,65},{65,129},{129,193},{2,66},{66,130... | collective-permute-start | bytes 393224 | tf_op jit(solution)/shard_map/ppermute | solution.py:151
  6.2 1.3 collective-permute-start.1
  7.5 1.5 fusion.206
  9.2 3.4 %collective-permute-done.1 = bf16[32,1,16,128]{3,0,2,1:T(8,128)(2,1)S(1)} collective-permute-done((bf16[32,1,16,128]{3,0,2,1:T(8,128)(2,1)S(1)}, bf16[32,1,16,128]{3,0,2,1:T(8,128)(2,1)S(1)}, u32[]{:S(2)}, u32[]{:S(2)}) %collective-permute-start.1) | collective-permute-done | bytes 131104 | tf_op jit(solution)/shard_map/ppermute | solution.py:153
  12.6 1.3 collective-permute-start.3
  13.9 4.0 %collective-permute-start.2 = (bf16[32,4,1,128]{3,0,2,1:T(8,128)(2,1)S(1)}, bf16[32,4,1,128]{3,0,2,1:T(8,128)(2,1)S(1)}, u32[]{:S(2)}, u32[]{:S(2)}) collective-permute-start(bf16[32,4,1,128]{3,0,2,1:T(8,128)(2,1)S(1)} %get-tuple-element.136), channel_id=1, source_target_pairs={{0,8},{8,16},{16,24},{24,32},{32,40},{40,48},{48,56},{1,9},{9,17},... | collective-permute-start | bytes 98312 | tf_op jit(solution)/shard_map/ppermute | solution.py:151
  19.7 5.9 %collective-permute-start.4 = (bf16[32,4,18,1]{0,1,3,2:T(4,128)(2,1)S(1)}, bf16[32,4,18,1]{0,1,3,2:T(4,128)(2,1)S(1)}, u32[]{:S(2)}, u32[]{:S(2)}) collective-permute-start(bf16[32,4,18,1]{0,1,3,2:T(4,128)(2,1)S(1)} %copy.119), channel_id=1, source_target_pairs={{0,1},{1,2},{2,3},{3,4},{4,5},{5,6},{6,7},{8,9},{9,10},{10,11},{11... | collective-permute-start | bytes 13832 | tf_op jit(solution)/shard_map/ppermute | solution.py:151
  26.1 1.9 collective-permute-start.5
  28.7 2.5 %collective-permute-done.5 = bf16[32,4,18,1]{0,1,3,2:T(4,128)(2,1)S(1)} collective-permute-done((bf16[32,4,18,1]{0,1,3,2:T(4,128)(2,1)S(1)}, bf16[32,4,18,1]{0,1,3,2:T(4,128)(2,1)S(1)}, u32[]{:S(2)}, u32[]{:S(2)}) %collective-permute-start.5) | collective-permute-done | bytes 4640 | tf_op jit(solution)/shard_map/ppermute | solution.py:153
  42.7 1.4 collective-permute-start.7
  44.1 4.2 %collective-permute-start.6 = (bf16[2,32,1,16,128]{4,1,3,2,0:T(8,128)(2,1)S(1)}, bf16[2,32,1,16,128]{4,1,3,2,0:T(8,128)(2,1)S(1)}, u32[]{:S(2)}, u32[]{:S(2)}) collective-permute-start(bf16[2,32,1,16,128]{4,1,3,2,0:T(8,128)(2,1)S(1)} %get-tuple-element.132), channel_id=1, source_target_pairs={{0,64},{64,128},{128,192},{1,65},{65,129},{129,193},{2,66},{66,130... | collective-permute-start | bytes 786440 | tf_op jit(solution)/shard_map/ppermute | solution.py:151
  49.8 1.4 collective-permute-done.7
  51.2 1.8 collective-permute-done.6
  53.0 1.3 collective-permute-start.9
  54.3 5.2 %collective-permute-start.8 = (bf16[2,32,4,1,128]{4,1,3,2,0:T(8,128)(2,1)S(1)}, bf16[2,32,4,1,128]{4,1,3,2,0:T(8,128)(2,1)}, u32[]{:S(2)}, u32[]{:S(2)}) collective-permute-start(bf16[2,32,4,1,128]{4,1,3,2,0:T(8,128)(2,1)S(1)} %get-tuple-element.108), channel_id=1, source_target_pairs={{0,8},{8,16},{16,24},{24,32},{32,40},{40,48},{48,56},{1,9},{9,17},... | collective-permute-start | bytes 196616 | tf_op jit(solution)/shard_map/ppermute | solution.py:151
  61.8 1.5 copy.145
  63.4 1.9 collective-permute-start.11
  66.2 5.0 %collective-permute-start.10 = (bf16[2,32,4,18,1]{1,2,4,3,0:T(4,128)(2,1)S(1)}, bf16[2,32,4,18,1]{1,2,4,3,0:T(4,128)(2,1)}, u32[]{:S(2)}, u32[]{:S(2)}) collective-permute-start(bf16[2,32,4,18,1]{1,2,4,3,0:T(4,128)(2,1)S(1)} %copy.144), channel_id=1, source_target_pairs={{0,1},{1,2},{2,3},{3,4},{4,5},{5,6},{6,7},{8,9},{9,10},{10,11},{11... | collective-permute-start | bytes 27656 | tf_op jit(solution)/shard_map/ppermute | solution.py:151
  79.5 1.7 copy.146
  81.2 3.8 %pad_maximum_fusion = bf16[2,32,4,18,130]{4,1,3,2,0:T(8,128)(2,1)S(1)} fusion(bf16[2,32,4,18,1]{4,1,3,2,0:T(8,128)(2,1)S(1)} %copy.147, bf16[2,32,4,1,128]{4,1,3,2,0:T(8,128)(2,1)S(1)} %collective-permute-done.9, bf16[2,32,1,16,128]{4,1,3,2,0:T(8,128)(2,1)} %copy-done, bf16[1,32,2,16,128]{4,1,3,2,0:T(8,128)(2,1)S(1)} %fusion.10, ...), kind=kLoop, calls=%fused_computation | loop fusion | flops 9584640 | bytes 2396160 | tf_op jit(solution)/shard_map/concatenate | solution.py:149
  85.8 1.2 fusion.191
  87.5 1.2 fusion.189
  100.3 1.3 collective-permute-start.13
  101.6 4.4 %collective-permute-start.12 = (bf16[32,1,16,128]{3,0,2,1:T(8,128)(2,1)S(1)}, bf16[32,1,16,128]{3,0,2,1:T(8,128)(2,1)S(1)}, u32[]{:S(2)}, u32[]{:S(2)}) collective-permute-start(bf16[32,1,16,128]{3,0,2,1:T(8,128)(2,1)S(1)} %get-tuple-element.138), channel_id=1, source_target_pairs={{0,64},{64,128},{128,192},{1,65},{65,129},{129,193},{2,66},{66,130... | collective-permute-start | bytes 393224 | tf_op jit(solution)/shard_map/ppermute | solution.py:151
  106.5 1.6 collective-permute-done.12
  108.1 1.3 collective-permute-start.15
  109.4 5.1 %collective-permute-start.14 = (bf16[32,4,1,128]{3,0,2,1:T(8,128)(2,1)S(1)}, bf16[32,4,1,128]{3,0,2,1:T(8,128)(2,1)S(1)}, u32[]{:S(2)}, u32[]{:S(2)}) collective-permute-start(bf16[32,4,1,128]{3,0,2,1:T(8,128)(2,1)S(1)} %get-tuple-element.130), channel_id=1, source_target_pairs={{0,8},{8,16},{16,24},{24,32},{32,40},{40,48},{48,56},{1,9},{9,17},... | collective-permute-start | bytes 98312 | tf_op jit(solution)/shard_map/ppermute | solution.py:151
  116.8 4.4 %collective-permute-start.16 = (bf16[32,4,18,1]{0,1,3,2:T(4,128)(2,1)S(1)}, bf16[32,4,18,1]{0,1,3,2:T(4,128)(2,1)S(1)}, u32[]{:S(2)}, u32[]{:S(2)}) collective-permute-start(bf16[32,4,18,1]{0,1,3,2:T(4,128)(2,1)S(1)} %copy.166), channel_id=1, source_target_pairs={{0,1},{1,2},{2,3},{3,4},{4,5},{5,6},{6,7},{8,9},{9,10},{10,11},{11... | collective-permute-start | bytes 13832 | tf_op jit(solution)/shard_map/ppermute | solution.py:151
  121.7 1.9 collective-permute-start.17
  127.3 1.4 maximum_maximum_fusion.1
  142.3 1.4 convolution_bitcast_fusion.10
  147.3 54.3 %shard_map.76 = f32[8,2,4,8,128]{4,3,2,1,0:T(8,128)} custom-call(f32[8,2,4,8,128]{4,3,2,1,0:T(8,128)} %bitcast.373), custom_call_target="tpu_custom_call" | custom-call | tf_op jit(solution)/shard_map/pallas_call | solution.py:121
  (401 shorter events, 68.2 us)
Async XLA Ops:
  0.6 8.4 %copy-start.2 = (bf16[32,2,16,128]{3,2,1,0:T(8,128)(2,1)S(1)}, bf16[32,2,16,128]{3,2,1,0:T(8,128)(2,1)}, u32[]{:S(2)}) copy-start(bf16[32,2,16,128]{3,2,1,0:T(8,128)(2,1)} %param.5) | copy-start | bytes 786436
  0.6 17.2 %copy-start.6 = (bf16[3,3,3,32,32]{4,3,2,1,0:T(8,128)(2,1)S(1)}, bf16[3,3,3,32,32]{4,3,2,1,0:T(8,128)(2,1)}, u32[]{:S(2)}) copy-start(bf16[3,3,3,32,32]{4,3,2,1,0:T(8,128)(2,1)} %param.8) | copy-start | bytes 165892
  1.8 39.6 %copy-start.3 = (bf16[32,2,16,128]{3,0,2,1:T(8,128)(2,1)}, bf16[32,2,16,128]{3,0,2,1:T(8,128)(2,1)S(1)}, u32[]{:S(2)}) copy-start(bf16[32,2,16,128]{3,0,2,1:T(8,128)(2,1)S(1)} %copy.116) | copy-start | bytes 786436
  1.8 7.2 %collective-permute-start = (bf16[32,1,16,128]{3,0,2,1:T(8,128)(2,1)S(1)}, bf16[32,1,16,128]{3,0,2,1:T(8,128)(2,1)S(1)}, u32[]{:S(2)}, u32[]{:S(2)}) collective-permute-start(bf16[32,1,16,128]{3,0,2,1:T(8,128)(2,1)S(1)} %get-tuple-element.141), channel_id=1, source_target_pairs={{0,64},{64,128},{128,192},{1,65},{65,129},{129,193},{2,66},{66,130... | collective-permute-start | bytes 393224 | tf_op jit(solution)/shard_map/ppermute | solution.py:151
  6.2 6.4 %collective-permute-start.1 = (bf16[32,1,16,128]{3,0,2,1:T(8,128)(2,1)S(1)}, bf16[32,1,16,128]{3,0,2,1:T(8,128)(2,1)S(1)}, u32[]{:S(2)}, u32[]{:S(2)}) collective-permute-start(bf16[32,1,16,128]{3,0,2,1:T(8,128)(2,1)S(1)} %get-tuple-element.140), channel_id=1, source_target_pairs={{64,0},{128,64},{192,128},{65,1},{129,65},{193,129},{66,2},{130,66... | collective-permute-start | bytes 393224 | tf_op jit(solution)/shard_map/ppermute | solution.py:153
  9.0 29.9 %copy-start.62 = (bf16[32,1,16,128]{3,0,2,1:T(8,128)(2,1)}, bf16[32,1,16,128]{3,0,2,1:T(8,128)(2,1)S(1)}, u32[]{:S(2)}) copy-start(bf16[32,1,16,128]{3,0,2,1:T(8,128)(2,1)S(1)} %collective-permute-done) | copy-start | bytes 393220
  12.6 6.0 %collective-permute-start.3 = (bf16[32,4,1,128]{3,0,2,1:T(8,128)(2,1)S(1)}, bf16[32,4,1,128]{3,0,2,1:T(8,128)(2,1)S(1)}, u32[]{:S(2)}, u32[]{:S(2)}) collective-permute-start(bf16[32,4,1,128]{3,0,2,1:T(8,128)(2,1)S(1)} %get-tuple-element.137), channel_id=1, source_target_pairs={{8,0},{16,8},{24,16},{32,24},{40,32},{48,40},{56,48},{9,1},{17,9},... | collective-permute-start | bytes 98312 | tf_op jit(solution)/shard_map/ppermute | solution.py:153
  13.9 5.0 %collective-permute-start.2 = (bf16[32,4,1,128]{3,0,2,1:T(8,128)(2,1)S(1)}, bf16[32,4,1,128]{3,0,2,1:T(8,128)(2,1)S(1)}, u32[]{:S(2)}, u32[]{:S(2)}) collective-permute-start(bf16[32,4,1,128]{3,0,2,1:T(8,128)(2,1)S(1)} %get-tuple-element.136), channel_id=1, source_target_pairs={{0,8},{8,16},{16,24},{24,32},{32,40},{40,48},{48,56},{1,9},{9,17},... | collective-permute-start | bytes 98312 | tf_op jit(solution)/shard_map/ppermute | solution.py:151
  19.7 8.4 %collective-permute-start.4 = (bf16[32,4,18,1]{0,1,3,2:T(4,128)(2,1)S(1)}, bf16[32,4,18,1]{0,1,3,2:T(4,128)(2,1)S(1)}, u32[]{:S(2)}, u32[]{:S(2)}) collective-permute-start(bf16[32,4,18,1]{0,1,3,2:T(4,128)(2,1)S(1)} %copy.119), channel_id=1, source_target_pairs={{0,1},{1,2},{2,3},{3,4},{4,5},{5,6},{6,7},{8,9},{9,10},{10,11},{11... | collective-permute-start | bytes 13832 | tf_op jit(solution)/shard_map/ppermute | solution.py:151
  26.1 5.1 %collective-permute-start.5 = (bf16[32,4,18,1]{0,1,3,2:T(4,128)(2,1)S(1)}, bf16[32,4,18,1]{0,1,3,2:T(4,128)(2,1)S(1)}, u32[]{:S(2)}, u32[]{:S(2)}) collective-permute-start(bf16[32,4,18,1]{0,1,3,2:T(4,128)(2,1)S(1)} %copy.121), channel_id=1, source_target_pairs={{1,0},{2,1},{3,2},{4,3},{5,4},{6,5},{7,6},{9,8},{10,9},{11,10},{12... | collective-permute-start | bytes 13832 | tf_op jit(solution)/shard_map/ppermute | solution.py:153
  28.1 10.3 %copy-start.12 = (bf16[32,2,16,128]{3,0,2,1:T(8,128)(2,1)}, bf16[32,2,16,128]{3,0,2,1:T(8,128)(2,1)S(1)}, u32[]{:S(2)}) copy-start(bf16[32,2,16,128]{3,0,2,1:T(8,128)(2,1)S(1)} %get-tuple-element.134) | copy-start | bytes 786436
  28.1 11.1 %copy-start.14 = (bf16[32,2,16,128]{3,0,2,1:T(8,128)(2,1)}, bf16[32,2,16,128]{3,0,2,1:T(8,128)(2,1)S(1)}, u32[]{:S(2)}) copy-start(bf16[32,2,16,128]{3,0,2,1:T(8,128)(2,1)S(1)} %get-tuple-element.125) | copy-start | bytes 786436
  28.1 11.8 %copy-start.20 = (bf16[32,2,16,128]{3,0,2,1:T(8,128)(2,1)}, bf16[32,2,16,128]{3,0,2,1:T(8,128)(2,1)S(1)}, u32[]{:S(2)}) copy-start(bf16[32,2,16,128]{3,0,2,1:T(8,128)(2,1)S(1)} %get-tuple-element.135) | copy-start | bytes 786436
  28.1 12.5 %copy-start.22 = (bf16[32,2,16,128]{3,0,2,1:T(8,128)(2,1)}, bf16[32,2,16,128]{3,0,2,1:T(8,128)(2,1)S(1)}, u32[]{:S(2)}) copy-start(bf16[32,2,16,128]{3,0,2,1:T(8,128)(2,1)S(1)} %get-tuple-element.124) | copy-start | bytes 786436
  33.7 7.6 %copy-start.28 = (bf16[32,2,16,128]{3,0,2,1:T(8,128)(2,1)}, bf16[32,2,16,128]{3,0,2,1:T(8,128)(2,1)S(1)}, u32[]{:S(2)}) copy-start(bf16[32,2,16,128]{3,0,2,1:T(8,128)(2,1)S(1)} %get-tuple-element.91) | copy-start | bytes 786436
  33.7 7.6 %copy-start.30 = (bf16[32,2,16,128]{3,0,2,1:T(8,128)(2,1)}, bf16[32,2,16,128]{3,0,2,1:T(8,128)(2,1)S(1)}, u32[]{:S(2)}) copy-start(bf16[32,2,16,128]{3,0,2,1:T(8,128)(2,1)S(1)} %get-tuple-element.194) | copy-start | bytes 786436
  33.8 8.2 %copy-start.32 = (bf16[32,2,16,128]{3,0,2,1:T(8,128)(2,1)}, bf16[32,2,16,128]{3,0,2,1:T(8,128)(2,1)S(1)}, u32[]{:S(2)}) copy-start(bf16[32,2,16,128]{3,0,2,1:T(8,128)(2,1)S(1)} %get-tuple-element.90) | copy-start | bytes 786436
  33.8 8.2 %copy-start.34 = (bf16[32,2,16,128]{3,0,2,1:T(8,128)(2,1)}, bf16[32,2,16,128]{3,0,2,1:T(8,128)(2,1)S(1)}, u32[]{:S(2)}) copy-start(bf16[32,2,16,128]{3,0,2,1:T(8,128)(2,1)S(1)} %get-tuple-element.195) | copy-start | bytes 786436
  42.7 8.5 %collective-permute-start.7 = (bf16[2,32,1,16,128]{4,1,3,2,0:T(8,128)(2,1)S(1)}, bf16[2,32,1,16,128]{4,1,3,2,0:T(8,128)(2,1)S(1)}, u32[]{:S(2)}, u32[]{:S(2)}) collective-permute-start(bf16[2,32,1,16,128]{4,1,3,2,0:T(8,128)(2,1)S(1)} %get-tuple-element.133), channel_id=1, source_target_pairs={{64,0},{128,64},{192,128},{65,1},{129,65},{193,129},{66,2},{130,66... | collective-permute-start | bytes 786440 | tf_op jit(solution)/shard_map/ppermute | solution.py:153
  44.1 8.9 %collective-permute-start.6 = (bf16[2,32,1,16,128]{4,1,3,2,0:T(8,128)(2,1)S(1)}, bf16[2,32,1,16,128]{4,1,3,2,0:T(8,128)(2,1)S(1)}, u32[]{:S(2)}, u32[]{:S(2)}) collective-permute-start(bf16[2,32,1,16,128]{4,1,3,2,0:T(8,128)(2,1)S(1)} %get-tuple-element.132), channel_id=1, source_target_pairs={{0,64},{64,128},{128,192},{1,65},{65,129},{129,193},{2,66},{66,130... | collective-permute-start | bytes 786440 | tf_op jit(solution)/shard_map/ppermute | solution.py:151
  51.2 9.0 %copy-start = (bf16[2,32,1,16,128]{4,1,3,2,0:T(8,128)(2,1)}, bf16[2,32,1,16,128]{4,1,3,2,0:T(8,128)(2,1)S(1)}, u32[]{:S(2)}) copy-start(bf16[2,32,1,16,128]{4,1,3,2,0:T(8,128)(2,1)S(1)} %collective-permute-done.7) | copy-start | bytes 786436
  53.0 7.2 %collective-permute-start.9 = (bf16[2,32,4,1,128]{4,1,3,2,0:T(8,128)(2,1)S(1)}, bf16[2,32,4,1,128]{4,1,3,2,0:T(8,128)(2,1)S(1)}, u32[]{:S(2)}, u32[]{:S(2)}) collective-permute-start(bf16[2,32,4,1,128]{4,1,3,2,0:T(8,128)(2,1)S(1)} %get-tuple-element.109), channel_id=1, source_target_pairs={{8,0},{16,8},{24,16},{32,24},{40,32},{48,40},{56,48},{9,1},{17,9},... | collective-permute-start | bytes 196616 | tf_op jit(solution)/shard_map/ppermute | solution.py:153
  54.3 5.9 %collective-permute-start.8 = (bf16[2,32,4,1,128]{4,1,3,2,0:T(8,128)(2,1)S(1)}, bf16[2,32,4,1,128]{4,1,3,2,0:T(8,128)(2,1)}, u32[]{:S(2)}, u32[]{:S(2)}) collective-permute-start(bf16[2,32,4,1,128]{4,1,3,2,0:T(8,128)(2,1)S(1)} %get-tuple-element.108), channel_id=1, source_target_pairs={{0,8},{8,16},{16,24},{24,32},{32,40},{40,48},{48,56},{1,9},{9,17},... | collective-permute-start | bytes 196616 | tf_op jit(solution)/shard_map/ppermute | solution.py:151
  63.4 15.1 %collective-permute-start.11 = (bf16[2,32,4,18,1]{1,2,4,3,0:T(4,128)(2,1)}, bf16[2,32,4,18,1]{1,2,4,3,0:T(4,128)(2,1)S(1)}, u32[]{:S(2)}, u32[]{:S(2)}) collective-permute-start(bf16[2,32,4,18,1]{1,2,4,3,0:T(4,128)(2,1)} %copy.145), channel_id=1, source_target_pairs={{1,0},{2,1},{3,2},{4,3},{5,4},{6,5},{7,6},{9,8},{10,9},{11,10},{12... | collective-permute-start | bytes 27656 | tf_op jit(solution)/shard_map/ppermute | solution.py:153
  66.2 13.3 %collective-permute-start.10 = (bf16[2,32,4,18,1]{1,2,4,3,0:T(4,128)(2,1)S(1)}, bf16[2,32,4,18,1]{1,2,4,3,0:T(4,128)(2,1)}, u32[]{:S(2)}, u32[]{:S(2)}) collective-permute-start(bf16[2,32,4,18,1]{1,2,4,3,0:T(4,128)(2,1)S(1)} %copy.144), channel_id=1, source_target_pairs={{0,1},{1,2},{2,3},{3,4},{4,5},{5,6},{6,7},{8,9},{9,10},{10,11},{11... | collective-permute-start | bytes 27656 | tf_op jit(solution)/shard_map/ppermute | solution.py:151
  100.3 6.2 %collective-permute-start.13 = (bf16[32,1,16,128]{3,0,2,1:T(8,128)(2,1)S(1)}, bf16[32,1,16,128]{3,0,2,1:T(8,128)(2,1)S(1)}, u32[]{:S(2)}, u32[]{:S(2)}) collective-permute-start(bf16[32,1,16,128]{3,0,2,1:T(8,128)(2,1)S(1)} %get-tuple-element.139), channel_id=1, source_target_pairs={{64,0},{128,64},{192,128},{65,1},{129,65},{193,129},{66,2},{130,66... | collective-permute-start | bytes 393224 | tf_op jit(solution)/shard_map/ppermute | solution.py:153
  101.6 6.5 %collective-permute-start.12 = (bf16[32,1,16,128]{3,0,2,1:T(8,128)(2,1)S(1)}, bf16[32,1,16,128]{3,0,2,1:T(8,128)(2,1)S(1)}, u32[]{:S(2)}, u32[]{:S(2)}) collective-permute-start(bf16[32,1,16,128]{3,0,2,1:T(8,128)(2,1)S(1)} %get-tuple-element.138), channel_id=1, source_target_pairs={{0,64},{64,128},{128,192},{1,65},{65,129},{129,193},{2,66},{66,130... | collective-permute-start | bytes 393224 | tf_op jit(solution)/shard_map/ppermute | solution.py:151
  108.1 7.8 %collective-permute-start.15 = (bf16[32,4,1,128]{3,0,2,1:T(8,128)(2,1)S(1)}, bf16[32,4,1,128]{3,0,2,1:T(8,128)(2,1)S(1)}, u32[]{:S(2)}, u32[]{:S(2)}) collective-permute-start(bf16[32,4,1,128]{3,0,2,1:T(8,128)(2,1)S(1)} %get-tuple-element.131), channel_id=1, source_target_pairs={{8,0},{16,8},{24,16},{32,24},{40,32},{48,40},{56,48},{9,1},{17,9},... | collective-permute-start | bytes 98312 | tf_op jit(solution)/shard_map/ppermute | solution.py:153
  109.4 6.5 %collective-permute-start.14 = (bf16[32,4,1,128]{3,0,2,1:T(8,128)(2,1)S(1)}, bf16[32,4,1,128]{3,0,2,1:T(8,128)(2,1)S(1)}, u32[]{:S(2)}, u32[]{:S(2)}) collective-permute-start(bf16[32,4,1,128]{3,0,2,1:T(8,128)(2,1)S(1)} %get-tuple-element.130), channel_id=1, source_target_pairs={{0,8},{8,16},{16,24},{24,32},{32,40},{40,48},{48,56},{1,9},{9,17},... | collective-permute-start | bytes 98312 | tf_op jit(solution)/shard_map/ppermute | solution.py:151
  116.8 9.0 %collective-permute-start.16 = (bf16[32,4,18,1]{0,1,3,2:T(4,128)(2,1)S(1)}, bf16[32,4,18,1]{0,1,3,2:T(4,128)(2,1)S(1)}, u32[]{:S(2)}, u32[]{:S(2)}) collective-permute-start(bf16[32,4,18,1]{0,1,3,2:T(4,128)(2,1)S(1)} %copy.166), channel_id=1, source_target_pairs={{0,1},{1,2},{2,3},{3,4},{4,5},{5,6},{6,7},{8,9},{9,10},{10,11},{11... | collective-permute-start | bytes 13832 | tf_op jit(solution)/shard_map/ppermute | solution.py:151
  121.7 5.1 %collective-permute-start.17 = (bf16[32,4,18,1]{0,1,3,2:T(4,128)(2,1)S(1)}, bf16[32,4,18,1]{0,1,3,2:T(4,128)(2,1)S(1)}, u32[]{:S(2)}, u32[]{:S(2)}) collective-permute-start(bf16[32,4,18,1]{0,1,3,2:T(4,128)(2,1)S(1)} %copy.168), channel_id=1, source_target_pairs={{1,0},{2,1},{3,2},{4,3},{5,4},{6,5},{7,6},{9,8},{10,9},{11,10},{12... | collective-permute-start | bytes 13832 | tf_op jit(solution)/shard_map/ppermute | solution.py:153
  146.5 57.1 %copy-start.7 = (bf16[3,3,3,32,32]{4,3,2,1,0:T(8,128)(2,1)S(1)}, bf16[3,3,3,32,32]{4,3,2,1,0:T(8,128)(2,1)}, u32[]{:S(2)}) copy-start(bf16[3,3,3,32,32]{4,3,2,1,0:T(8,128)(2,1)} %param.8) | copy-start | bytes 165892
  (98 other events, 193.8 us)

commit v2 on v1

v2 whole, which is shorter than its diff:
```python
import functools
import itertools
import math

import jax
import jax.numpy as jnp
from jax import lax
from jax.experimental import pallas as pl
from jax.experimental.pallas import tpu as pltpu
from jax.sharding import PartitionSpec as P

MESH = pl.DeviceIdType.MESH
BF16 = jnp.bfloat16
F32 = jnp.float32
OFFSETS = [o for o in itertools.product((-1, 0, 1), repeat=3) if o != (0, 0, 0)]
SIDES = [(ox, oz) for ox in (-1, 0, 1) for oz in (-1, 1)]


def gelu_pair(pre):
    square = pre * pre
    hyper = jnp.tanh(0.7978845608 * (pre + 0.044715 * square * pre))
    half = 0.5 * (1.0 + hyper)
    hidden = pre * half
    slope = half + (0.5 * pre) * (1.0 - hyper * hyper) * (0.7978845608 * (1.0 + 0.134145 * square))
    return (hidden, slope)


def main_kernel(
    nx, ny, nz, dx, dy, tiles, share,
    vol, w_first, w_second, v_first, v_second,
    tot, jv_out,
    a1, a2, a3, slope_ref, ej, eb, w1t, w2t, w3t,
    pk1, ed1, pk2, ed2, pk3, ed3,
    part, recv1, rows, recv2, gath, chunk,
    xs1, xr1, xs2, xr2, xs3, xr3, ps3, pr3,
    s1, r1, s2, r2, s3, r3, s4, r4,
):
    ix, iy, iz = lax.axis_index("gx"), lax.axis_index("gy"), lax.axis_index("gz")
    plane = nx * ny
    me = iy * nx + ix
    chan = vol.shape[0]
    hx, hy = dx + 2, dy + 4
    lane = lax.broadcasted_iota(jnp.int32, (chan, 128), 1)

    def there(ox, oy, oz):
        ok = None
        for offset, index, count in ((ox, ix, nx), (oy, iy, ny), (oz, iz, nz)):
            if offset:
                one = index < count - 1 if offset > 0 else index > 0
                ok = one if ok is None else jnp.logical_and(ok, one)
        return ok

    def at(ox, oy, oz):
        return {"gx": ix + ox, "gy": iy + oy, "gz": iz + oz}

    def z_peer(d):
        return {"gx": ix, "gy": iy, "gz": lax.rem(iz + d, nz)}

    def p_peer(d):
        q = lax.rem(me + d, plane)
        return q, {"gx": lax.rem(q, nx), "gy": q // nx, "gz": iz}

    barrier = pltpu.get_barrier_semaphore()
    for o in OFFSETS:
        @pl.when(there(*o))
        def _():
            pl.semaphore_signal(barrier, inc=1, device_id=at(*o), device_id_type=MESH)
    for d in range(1, nz):
        pl.semaphore_signal(barrier, inc=1, device_id=z_peer(d), device_id_type=MESH)

    def greet(d, _):
        pl.semaphore_signal(barrier, inc=1, device_id=p_peer(d)[1], device_id_type=MESH)
        return 0

    lax.fori_loop(1, plane, greet, 0)

    taps = w_first.shape[0]
    w1t[...] = jnp.zeros(w1t.shape, BF16)
    w2t[...] = jnp.zeros(w2t.shape, BF16)
    w3t[...] = jnp.zeros(w3t.shape, BF16)
    w1t[0:chan, 0:taps] = w_first[...].T
    w1t[chan : 2 * chan, 0:taps] = v_first[...].T
    w2t[:, 0:taps] = w_second[...].T
    w2t[:, 896 : 896 + taps] = v_second[...].T
    for k in range(27):
        w3t[:, chan * k : chan * (k + 1)] = w_second[chan * (26 - k) : chan * (27 - k), :]

    def zero(ref):
        ref[...] = jnp.zeros(ref.shape, ref.dtype)

    for x in range(dx):
        a1[dx + x, 3 : 3 + dy, chan : 2 * chan, :] = jnp.transpose(vol[:, x], (1, 0, 2))
        zero(ej.at[x, 0:3])
        zero(ej.at[x, 3 + dy : 5 + dy])
        zero(eb.at[x, 0:3])
        zero(eb.at[x, 3 + dy : 5 + dy])

    def packed(raw, j, pair):
        first = jnp.where(lane == j, jnp.broadcast_to(raw[:, 0:1], raw.shape), pair[0])
        last = jnp.where(lane == j, jnp.broadcast_to(raw[:, 127:128], raw.shape), pair[1])
        return first, last

    blank = jnp.zeros((chan, 128), BF16)

    def pack1(j, pair):
        return packed(a1[dx + j // dy, 3 + lax.rem(j, dy), chan : 2 * chan, :], j, pair)

    pk1[0], pk1[1] = lax.fori_loop(0, dx * dy, pack1, (blank, blank), unroll=4)

    @pl.when(ix == 0)
    def _():
        for x in range(dx):
            zero(a1.at[x, :, chan : 2 * chan, :])
        zero(ed1.at[:, 0])
        zero(a3.at[0])
        zero(ed3.at[:, 0])

    @pl.when(ix == nx - 1)
    def _():
        for x in range(dx):
            zero(a1.at[2 * dx + x, :, chan : 2 * chan, :])
        zero(ed1.at[:, 2])
        zero(a3.at[dx + 1])
        zero(ed3.at[:, 2])

    @pl.when(iy == 0)
    def _():
        for x in range(3 * dx):
            zero(a1.at[x, 0:3, chan : 2 * chan, :])
        zero(ed1.at[:, :, 0])

    @pl.when(iy == ny - 1)
    def _():
        for x in range(3 * dx):
            zero(a1.at[x, 3 + dy : 6 + dy, chan : 2 * chan, :])
        zero(ed1.at[:, :, 2])

    @pl.when(iz == 0)
    def _():
        zero(ed1.at[0])
        zero(ed2.at[0])
        zero(ed3.at[0])

    @pl.when(iz == nz - 1)
    def _():
        zero(ed1.at[1])
        zero(ed2.at[1])
        zero(ed3.at[1])

    def span(index, count):
        return 3 - (index == 0).astype(jnp.int32) - (index == count - 1).astype(jnp.int32)

    near = span(ix, nx) * span(iy, ny) * span(iz, nz) - 1
    pl.semaphore_wait(barrier, near + nz - 1 + plane - 1)

    def send_vol(n):
        ox, oy, oz = OFFSETS[n]
        if oz == 0:
            count = dy if oy == 0 else 3
            src_y = 3 if oy <= 0 else dy
            dst_y = 3 if oy == 0 else (0 if oy > 0 else 3 + dy)
            to_x = dx * (1 - ox)
            src = a1.at[dx : 2 * dx, src_y : src_y + count, chan : 2 * chan, :]
            dst = a1.at[to_x : to_x + dx, dst_y : dst_y + count, chan : 2 * chan, :]
        else:
            src = pk1.at[1 if oz > 0 else 0]
            dst = ed1.at[0 if oz > 0 else 1, 1 - ox, 1 - oy]
        return pltpu.make_async_remote_copy(
            src, dst, xs1.at[n], xr1.at[n], device_id=at(ox, oy, oz), device_id_type=MESH
        )

    for n, o in enumerate(OFFSETS):
        @pl.when(there(*o))
        def _():
            send_vol(n).start()
    for n, o in enumerate(OFFSETS):
        @pl.when(there(*(-c for c in o)))
        def _():
            send_vol(n).wait_recv()

    def shifted(raw, left, right, j):
        before = jnp.where(lane == 0, pltpu.roll(left, lax.rem(128 - j, 128), 1), pltpu.roll(raw, 1, 1))
        after = jnp.where(lane == 127, pltpu.roll(right, 127 - j, 1), pltpu.roll(raw, 127, 1))
        return before, after

    def slab1(i, _):
        x = i // (dy + 6)
        y = lax.rem(i, dy + 6)
        bx = x // dx
        by = (y + dy - 3) // dy
        j = lax.rem(x, dx) * dy + lax.rem(y + dy - 3, dy)
        raw = a1[x, y, chan : 2 * chan, :]
        before, after = shifted(raw, ed1[0, bx, by], ed1[1, bx, by], j)
        a1[x, y, 0:chan, :] = before
        a1[x, y, 2 * chan : 3 * chan, :] = after
        return 0

    lax.fori_loop(0, 3 * dx * (dy + 6), slab1, 0, unroll=4)

    def stacked(ref, x, y):
        halves = []
        for half in range(2):
            pieces = [ref[x + kx, y + half + ky] for kx in range(3) for ky in range(3)]
            pieces.append(ref[x, y + half, 0:chan, :])
            halves.append(jnp.concatenate(pieces, axis=0))
        return jnp.concatenate(halves, axis=1)

    pairs1 = hy // 2

    def layer1(i, carry):
        x = i // pairs1
        y = 2 * lax.rem(i, pairs1)
        both = jnp.dot(w1t[...], stacked(a1, x, y), preferred_element_type=F32)
        hidden, slope = gelu_pair(both[0:chan])
        gx_cell = ix * dx + x - 1
        gy_cell = iy * dy + y - 2
        inside = jnp.logical_and(
            jnp.logical_and(gx_cell >= 0, gx_cell < nx * dx), jnp.logical_and(gy_cell >= 0, gy_cell < ny * dy)
        )
        keep = inside.astype(F32)
        tangent = (keep * (slope * both[chan : 2 * chan])).astype(BF16)
        hidden = (keep * hidden).astype(BF16)
        fields = [carry[0:2], carry[2:4]]
        for half in range(2):
            cols = slice(128 * half, 128 * half + 128)
            for f, value in enumerate((tangent, hidden)):
                a2[f, x, y + half, chan : 2 * chan, :] = value[:, cols]
                fields[f] = packed(value[:, cols], x * hy + y + half, fields[f])
            slope_ref[x, y + half] = slope[:, cols]
        return (*fields[0], *fields[1])

    edges = lax.fori_loop(0, hx * pairs1, layer1, (blank,) * 4, unroll=2)
    pk2[0, 0], pk2[1, 0], pk2[0, 1], pk2[1, 1] = edges

    def send_hid(n, oz):
        return pltpu.make_async_remote_copy(
            pk2.at[n], ed2.at[1 - n], xs2.at[n], xr2.at[n], device_id=at(0, 0, oz), device_id_type=MESH
        )

    for n, oz in enumerate((-1, 1)):
        @pl.when(there(0, 0, oz))
        def _():
            send_hid(n, oz).start()
    for n, oz in enumerate((-1, 1)):
        @pl.when(there(0, 0, -oz))
        def _():
            send_hid(n, oz).wait_recv()

    def slab2(i, _):
        x = i // hy
        y = lax.rem(i, hy)
        for f in range(2):
            before, after = shifted(a2[f, x, y, chan : 2 * chan, :], ed2[0, f], ed2[1, f], i)
            a2[f, x, y, 0:chan, :] = before
            a2[f, x, y, 2 * chan : 3 * chan, :] = after
        return 0

    lax.fori_loop(0, hx * hy, slab2, 0, unroll=2)

    pairs2 = (dy + 2) // 2

    def layer2(i, carry):
        x = i // pairs2
        y = 2 * lax.rem(i, pairs2)
        both = jnp.concatenate([stacked(a2.at[0], x, y), stacked(a2.at[1], x, y)], axis=0)
        out = jnp.dot(w2t[...], both, preferred_element_type=F32)
        for half in range(2):
            gy_cell = iy * dy + y + half - 1
            keep = jnp.logical_and(gy_cell >= 0, gy_cell < ny * dy).astype(F32)
            value = (keep * out[:, 128 * half : 128 * half + 128]).astype(BF16)
            a3[x + 1, y + half, chan : 2 * chan, :] = value
            carry = packed(value, x * (dy + 2) + y + half, carry)
        return carry

    pk3[0], pk3[1] = lax.fori_loop(0, dx * pairs2, layer2, (blank, blank), unroll=2)

    def send_plane(n, ox):
        return pltpu.make_async_remote_copy(
            a3.at[1 if ox < 0 else dx, :, chan : 2 * chan, :],
            a3.at[dx + 1 if ox < 0 else 0, :, chan : 2 * chan, :],
            ps3.at[n], pr3.at[n], device_id=at(ox, 0, 0), device_id_type=MESH,
        )

    def send_jv(n):
        ox, oz = SIDES[n]
        return pltpu.make_async_remote_copy(
            pk3.at[1 if oz > 0 else 0], ed3.at[0 if oz > 0 else 1, 1 - ox],
            xs3.at[n], xr3.at[n], device_id=at(ox, 0, oz), device_id_type=MESH,
        )

    for n, ox in enumerate((-1, 1)):
        @pl.when(there(ox, 0, 0))
        def _():
            send_plane(n, ox).start()
    for n, (ox, oz) in enumerate(SIDES):
        @pl.when(there(ox, 0, oz))
        def _():
            send_jv(n).start()

    for x in range(dx):
        own = a3[x + 1, 1 : 1 + dy, chan : 2 * chan, :]
        ej[x, 3 : 3 + dy] = own
        jv_out[x] = own

    def correlate(read, e_ref):
        total = None
        for x in range(dx):
            lhs = jnp.concatenate(
                [
                    jnp.concatenate([read(x + kx, q) for kx in range(3)], axis=0)
                    for q in range(dy + 2)
                ],
                axis=1,
            )
            rhs = jnp.concatenate(
                [
                    jnp.concatenate([e_ref[x, q - ky + 3] for ky in range(4)], axis=0)
                    for q in range(dy + 2)
                ],
                axis=1,
            )
            product = lax.dot_general(lhs, rhs, (((1,), (1,)), ((), ())), preferred_element_type=F32)
            total = product if total is None else total + product
        return total

    lane8 = lax.broadcasted_iota(jnp.int32, (8, 128), 1)

    def put_part(f, value):
        for t in range(nz * tiles):
            if t < 27:
                j, s = t // 9, t % 9
                tail = pltpu.roll(value[216 + 8 * s : 224 + 8 * s], 96 - 32 * j, 1)
                part[t // tiles, f, t % tiles] = jnp.where(lane8 < 96, value[8 * t : 8 * t + 8], tail)
            else:
                part[t // tiles, f, t % tiles] = jnp.zeros((8, 128), F32)

    def send1(f, d):
        peer = z_peer(d)
        return pltpu.make_async_remote_copy(
            part.at[peer["gz"], f], recv1.at[d - 1, f], s1.at[f, d - 1], r1.at[f, d - 1],
            device_id=peer, device_id_type=MESH,
        )

    put_part(0, correlate(lambda x, q: a2[1, x, q + 1], ej))
    for d in range(1, nz):
        send1(0, d).start()

    for n, ox in enumerate((-1, 1)):
        @pl.when(there(-ox, 0, 0))
        def _():
            send_plane(n, ox).wait_recv()
    for n, (ox, oz) in enumerate(SIDES):
        @pl.when(there(-ox, 0, -oz))
        def _():
            send_jv(n).wait_recv()

    def slab3(i, _):
        x = i // (dy + 2)
        y = lax.rem(i, dy + 2)
        bx = (x + dx - 1) // dx
        j = lax.rem(x + dx - 1, dx) * (dy + 2) + y
        before, after = shifted(a3[x, y, chan : 2 * chan, :], ed3[0, bx], ed3[1, bx], j)
        a3[x, y, 0:chan, :] = before
        a3[x, y, 2 * chan : 3 * chan, :] = after
        return 0

    lax.fori_loop(0, hx * (dy + 2), slab3, 0, unroll=4)

    pairs3 = dy // 2

    def layer3(i, _):
        x = i // pairs3
        y = 2 * lax.rem(i, pairs3)
        out = jnp.dot(w3t[...], stacked(a3, x, y), preferred_element_type=F32)
        for half in range(2):
            value = slope_ref[x + 1, y + half + 2] * out[:, 128 * half : 128 * half + 128]
            eb[x, y + half + 3] = value.astype(BF16)
        return 0

    lax.fori_loop(0, dx * pairs3, layer3, 0, unroll=2)

    put_part(1, correlate(lambda x, q: a1[x + 1, q + 2], eb))
    for d in range(1, nz):
        send1(1, d).start()

    for f in range(2):
        total = part[iz, f]
        for d in range(1, nz):
            send1(f, d).wait_recv()
            total = total + recv1[d - 1, f]
        for r in range(plane * share):
            if r < 8 * tiles:
                rows[r // share, f * share + r % share : f * share + r % share + 1, :] = total[r // 8, r % 8 : r % 8 + 1, :]
            else:
                rows[r // share, f * share + r % share : f * share + r % share + 1, :] = jnp.zeros((1, 128), F32)

    def send2(d):
        q, peer = p_peer(d)
        return pltpu.make_async_remote_copy(
            rows.at[q], recv2.at[d - 1], s2.at[d - 1], r2.at[d - 1], device_id=peer, device_id_type=MESH
        )

    def send3(d):
        q, peer = p_peer(d)
        return pltpu.make_async_remote_copy(
            gath.at[me], gath.at[me], s3.at[d - 1], r3.at[d - 1], device_id=peer, device_id_type=MESH
        )

    def start2(d, _):
        send2(d).start()
        return 0

    def take2(d, acc):
        send2(d).wait_recv()
        return acc + recv2[d - 1]

    def start3(d, _):
        send3(d).start()
        return 0

    def take3(d, _):
        send3(d).wait_recv()
        return 0

    lax.fori_loop(1, plane, start2, 0)
    gath[me] = lax.fori_loop(1, plane, take2, rows[me])
    lax.fori_loop(1, plane, start3, 0)
    lax.fori_loop(1, plane, take3, 0)
    for f in range(2):
        for r in range(8 * tiles):
            chunk[f, r // 8, r % 8 : r % 8 + 1, :] = gath[r // share, f * share + r % share : f * share + r % share + 1, :]

    def send4(d):
        return pltpu.make_async_remote_copy(
            chunk, tot.at[iz], s4.at[d - 1], r4.at[d - 1], device_id=z_peer(d), device_id_type=MESH
        )

    for d in range(1, nz):
        send4(d).start()
    tot[iz] = chunk[...]
    for d in range(1, nz):
        send4(d).wait_recv()

    for n, o in enumerate(OFFSETS):
        @pl.when(there(*o))
        def _():
            send_vol(n).wait_send()
    for n, oz in enumerate((-1, 1)):
        @pl.when(there(0, 0, oz))
        def _():
            send_hid(n, oz).wait_send()
    for n, ox in enumerate((-1, 1)):
        @pl.when(there(ox, 0, 0))
        def _():
            send_plane(n, ox).wait_send()
    for n, (ox, oz) in enumerate(SIDES):
        @pl.when(there(ox, 0, oz))
        def _():
            send_jv(n).wait_send()
    for d in range(1, nz):
        send1(0, d).wait_send()
        send1(1, d).wait_send()
        send4(d).wait_send()

    def drain(d, _):
        send2(d).wait_send()
        send3(d).wait_send()
        return 0

    lax.fori_loop(1, plane, drain, 0)


def last_kernel(tiles, count_all, factor, tot, jv_raw, v_first, v_second, jv, gv_first, gv_second):
    for x in range(jv_raw.shape[0]):
        jv[:, x] = jnp.transpose(jv_raw[x], (1, 0, 2))
    for f, (v_ref, out) in enumerate(((v_second, gv_second), (v_first, gv_first))):
        tile = [tot[t // tiles, f, t % tiles] for t in range(27)]
        for kx in range(3):
            for ky in range(3):
                pieces = []
                for u in range(12 * kx, 12 * kx + 12):
                    if u < 27:
                        piece = tile[u] if ky == 0 else pltpu.roll(tile[u], 128 - 32 * ky, 1)
                    else:
                        piece = pltpu.roll(tile[9 * ky + u - 27], 32, 1)
                    pieces.append(piece[:, 0:32])
                k = 3 * kx + ky
                summed = jnp.concatenate(pieces, axis=0)
                base = v_ref[96 * k : 96 * k + 96, :].astype(F32)
                out[k] = factor * (summed / count_all + 0.1 * base)


def body(volume, w_first, w_second, v_first, v_second):
    chan, dx, dy, dz = volume.shape
    nx, ny, nz = lax.axis_size("gx"), lax.axis_size("gy"), lax.axis_size("gz")
    plane = nx * ny
    tiles = -(-27 // nz)
    share = -(-8 * tiles // plane)
    count_all = float(dx * dy * dz * nx * ny * nz)
    factor = math.sqrt(27.0 * chan)
    shape = w_first.shape
    flat = [w.reshape(27 * chan, chan) for w in (w_first, w_second, v_first, v_second)]
    vm = pl.BlockSpec(memory_space=pltpu.VMEM)
    dma = pltpu.SemaphoreType.DMA
    tot, jv_raw = pl.pallas_call(
        functools.partial(main_kernel, nx, ny, nz, dx, dy, tiles, share),
        out_shape=(
            jax.ShapeDtypeStruct((nz, 2, tiles, 8, 128), F32),
            jax.ShapeDtypeStruct((dx, dy, chan, 128), BF16),
        ),
        in_specs=[vm] * 5,
        out_specs=(vm, vm),
        scratch_shapes=[
            pltpu.VMEM((3 * dx, dy + 6, 3 * chan, 128), BF16),
            pltpu.VMEM((2, dx + 2, dy + 4, 3 * chan, 128), BF16),
            pltpu.VMEM((dx + 2, dy + 2, 3 * chan, 128), BF16),
            pltpu.VMEM((dx + 2, dy + 4, chan, 128), F32),
            pltpu.VMEM((dx, dy + 5, chan, 128), BF16),
            pltpu.VMEM((dx, dy + 5, chan, 128), BF16),
            pltpu.VMEM((2 * chan, 896), BF16),
            pltpu.VMEM((chan, 1792), BF16),
            pltpu.VMEM((chan, 896), BF16),
            pltpu.VMEM((2, chan, 128), BF16),
            pltpu.VMEM((2, 3, 3, chan, 128), BF16),
            pltpu.VMEM((2, 2, chan, 128), BF16),
            pltpu.VMEM((2, 2, chan, 128), BF16),
            pltpu.VMEM((2, chan, 128), BF16),
            pltpu.VMEM((2, 3, chan, 128), BF16),
            pltpu.VMEM((nz, 2, tiles, 8, 128), F32),
            pltpu.VMEM((nz - 1, 2, tiles, 8, 128), F32),
            pltpu.VMEM((plane, 2 * share, 128), F32),
            pltpu.VMEM((plane - 1, 2 * share, 128), F32),
            pltpu.VMEM((plane, 2 * share, 128), F32),
            pltpu.VMEM((2, tiles, 8, 128), F32),
            dma((26,)), dma((26,)),
            dma((2,)), dma((2,)),
            dma((6,)), dma((6,)),
            dma((2,)), dma((2,)),
            dma((2, nz - 1)), dma((2, nz - 1)),
            dma((plane - 1,)), dma((plane - 1,)),
            dma((plane - 1,)), dma((plane - 1,)),
            dma((nz - 1,)), dma((nz - 1,)),
        ],
        compiler_params=pltpu.CompilerParams(collective_id=0, has_side_effects=True),
        cost_estimate=pl.CostEstimate(flops=2000000000, bytes_accessed=2000000, transcendentals=400000),
    )(volume, *flat)
    jv, gv_first, gv_second = pl.pallas_call(
        functools.partial(last_kernel, tiles, count_all, factor),
        out_shape=(
            jax.ShapeDtypeStruct((chan, dx, dy, 128), BF16),
            jax.ShapeDtypeStruct((9, 3 * chan, chan), F32),
            jax.ShapeDtypeStruct((9, 3 * chan, chan), F32),
        ),
        in_specs=[vm] * 4,
        out_specs=(vm, vm, vm),
    )(tot, jv_raw, flat[2], flat[3])
    return (jv, gv_first.reshape(shape), gv_second.reshape(shape))


def solution(mesh):
    in_specs = (P(None, "gx", "gy", "gz"), P(), P(), P(), P())
    out_specs = (P(None, "gx", "gy", "gz"), P(), P())
    return jax.shard_map(body, mesh=mesh, in_specs=in_specs, out_specs=out_specs, check_vma=False)
```

time: 208 us -> 102 us (0.49); the launches traced: 205 us -> 102 us
  starting transfers between devices: 56.2 us -> 0 us
  local copies, waits for them, and re-layouts: 49.2 us -> 0 us
  Pallas kernels: 54.3 us -> 102 us
  matrix products: 21 us -> 0 us
  waiting for transfers between devices: 11.4 us -> 0 us
  other arithmetic: 10.9 us -> 0 us
    ppermute x18 -> x0, starting transfers between devices: 56.2 us -> none  [the longest x9 42.6 us: padded_2(): lax.ppermute(tail, axis, [(i, (i + 1) % count) for i in range(ends)])]
    pallas_call x1 -> x2, Pallas kernels: 54.3 us -> 102 us  [the longest x1 99.2 us: body(): pl.pallas_call(functools.partial(main_kernel, nx, ny, nz, dx, dy, tiles,...]
    dot_general x63 -> x0, matrix products: 21 us -> none  [the longest x45 12.7 us: stencil(): jnp.einsum('kxyz,ko->oxyz', stacked, matrix, preferred_element_type=jnp.f...]
    slice x35 -> x0, local copies, waits for them, and re-layouts: 17.7 us -> none  [the longest x9 7.4 us: stencil(): padded[:, shift_x:shift_x + depth, shift_y:shift_y + height, shift_z:shif...]
    unnamed x230 -> x0, local copies, waits for them, and re-layouts: 15 us -> none
    ppermute x18 -> x0, waiting for transfers between devices: 11.4 us -> none  [the longest x9 7.79 us: padded_2(): lax.ppermute(head, axis, [((i + 1) % count, i) for i in range(ends)])]
    another operation x31 -> x0, local copies, waits for them, and re-layouts: 8.66 us -> none  [the longest x9 6.14 us: stencil(): matrix = weight[shift_x, shift_y].reshape(3 * in_chan, out_chan)]
    concatenate x8 -> x0, other arithmetic: 7.43 us -> none  [padded_2(): jnp.concatenate([lax.ppermute(tail, axis, [(i, (i + 1) % count) for i in...]
  transfers between devices with their start and end apart: 18 -> 0, of which waited for: 7 -> 0; matrix products, arithmetic and copies ran while one was open for 10% -> 0% of each run, Pallas kernels for 0% -> 0%
where the time goes in v2:
time: 102 us
  Pallas kernels  102 us (100%)
    pallas_call x1, Pallas kernels, body(): pl.pallas_call(functools.partial(main_kernel, nx, ny, nz, dx, dy, tiles,...  99.2 us
    pallas_call x1, Pallas kernels, body(): pl.pallas_call(functools.partial(last_kernel, tiles, count_all, factor),...  2.41 us

profile of v2, /device:TPU:1, one launch (start us, length us, event | category | flops | bytes accessed | tf_op | source)
XLA Modules:
  0.0 102.2 jit_solution(16278812421530845834)
XLA Ops:
  0.6 99.2 %shard_map.76 = (f32[8,2,4,8,128]{4,3,2,1,0:T(8,128)}, bf16[2,16,32,128]{3,2,1,0:T(8,128)(2,1)}) custom-call(bf16[32,2,16,128]{3,2,1,0:T(8,128)(2,1)} %vol.1, bf16[864,32]{1,0:T(8,128)(2,1)} %bitcast.12, bf16[864,32]{1,0:T(8,128)(2,1)} %bitcast.13, bf16[864,32]{1,0:T(8,128)(2,1)} %bitcast.6, bf16[864,32]{1,0:T(8,128)(2,1)} %bitcast.8), custom_call_target="tpu_custom_call" | custom-call | flops 2000000000 | bytes 2000000 | tf_op jit(solution)/shard_map/pallas_call | solution.py:505
  99.8 2.4 %shard_map.77 = (bf16[32,2,16,128]{3,2,1,0:T(8,128)(2,1)}, f32[9,96,32]{2,1,0:T(8,128)}, f32[9,96,32]{2,1,0:T(8,128)}) custom-call(f32[8,2,4,8,128]{4,3,2,1,0:T(8,128)} %get-tuple-element.8.tot, bf16[2,16,32,128]{3,2,1,0:T(8,128)(2,1)} %get-tuple-element.9.jv_raw, bf16[864,32]{1,0:T(8,128)(2,1)} %bitcast.7, bf16[864,32]{1,0:T(8,128)(2,1)} %bitcast.9), custom_call_target="tpu_custom_call" | custom-call | tf_op jit(solution)/shard_map/pallas_call | solution.py:547

commit v3 on v2

v3 whole, which is shorter than its diff:
```python
import functools
import itertools
import math

import jax
import jax.numpy as jnp
from jax import lax
from jax.experimental import pallas as pl
from jax.experimental.pallas import tpu as pltpu
from jax.sharding import PartitionSpec as P

MESH = pl.DeviceIdType.MESH
BF16 = jnp.bfloat16
F32 = jnp.float32
OFFSETS = [o for o in itertools.product((-1, 0, 1), repeat=3) if o != (0, 0, 0)]
VOLUME = [((ox, 0, 0), False) for ox in (-1, 1)]
VOLUME += [((ox, 0, oz), False) for ox in (0, -1, 1) for oz in (-1, 1)]
VOLUME += [(o, False) for o in OFFSETS if o[1] != 0]
VOLUME += [((ox, 0, 0), True) for ox in (-1, 1)]
SIDES = [(ox, oz) for ox in (-1, 0, 1) for oz in (-1, 1)]


def gelu_pair(pre):
    square = pre * pre
    hyper = jnp.tanh(0.7978845608 * (pre + 0.044715 * square * pre))
    half = 0.5 * (1.0 + hyper)
    hidden = pre * half
    slope = half + (0.5 * pre) * (1.0 - hyper * hyper) * (0.7978845608 * (1.0 + 0.134145 * square))
    return (hidden, slope)


def main_kernel(
    nx, ny, nz, dx, dy, tiles, share,
    vol, w_first, w_second, v_first, v_second,
    tot, jv_out,
    r1, q1, r2, q2, r3, q3, slope_ref, acc3, ej, eb, w1t, w2t, w3t,
    pk1, ed1, pk2, ed2, pk3, ed3,
    part, recv1, rows, recv2, gath, chunk,
    xs1, xr1, xs2, xr2, xs3, xr3, ps3, pr3,
    as1, ar1, as2, ar2, as3, ar3, as4, ar4,
):
    ix, iy, iz = lax.axis_index("gx"), lax.axis_index("gy"), lax.axis_index("gz")
    me = iy * nx + ix
    chan = vol.shape[0]
    two = 2 * chan
    hx, hy = dx + 2, dy + 4
    lane = lax.broadcasted_iota(jnp.int32, (chan, 128), 1)

    def there(ox, oy, oz):
        ok = None
        for offset, index, count in ((ox, ix, nx), (oy, iy, ny), (oz, iz, nz)):
            if offset:
                one = index < count - 1 if offset > 0 else index > 0
                ok = one if ok is None else jnp.logical_and(ok, one)
        return ok

    def at(ox, oy, oz):
        return {"gx": ix + ox, "gy": iy + oy, "gz": iz + oz}

    zs = [lax.rem(iz + d, nz) for d in range(nz)]
    ys = [lax.rem(iy + d, ny) for d in range(ny)]
    xs = [lax.rem(ix + d, nx) for d in range(nx)]
    turns = [(ey, ex) for ey in range(ny) for ex in range(nx)][1:]

    def z_peer(d):
        return {"gx": ix, "gy": iy, "gz": zs[d]}

    def p_peer(n):
        ey, ex = turns[n]
        return {"gx": xs[ex], "gy": ys[ey], "gz": iz}

    def copy(src, dst, send, recv, peer):
        return pltpu.make_async_remote_copy(src, dst, send, recv, device_id=peer, device_id_type=MESH)

    def guarded(cond, action):
        @pl.when(cond)
        def _():
            action()

    barrier = pltpu.get_barrier_semaphore()

    def greet(peer):
        pl.semaphore_signal(barrier, inc=1, device_id=peer, device_id_type=MESH)

    for n in range(len(turns)):
        greet(p_peer(n))
    for o in OFFSETS:
        guarded(there(*o), lambda: greet(at(*o)))
    for d in range(1, nz):
        greet(z_peer(d))

    def zero(ref):
        ref[...] = jnp.zeros(ref.shape, ref.dtype)

    for x in range(dx):
        r1[dx + x, 3 : 3 + dy] = jnp.transpose(vol[:, x], (1, 0, 2))

    def packed(raw, j, pair):
        first = jnp.where(lane == j, jnp.broadcast_to(raw[:, 0:1], raw.shape), pair[0])
        last = jnp.where(lane == j, jnp.broadcast_to(raw[:, 127:128], raw.shape), pair[1])
        return first, last

    blank = jnp.zeros((chan, 128), BF16)
    edges = (blank, blank)
    for x in range(dx):
        for y in range(dy):
            edges = packed(r1[dx + x, 3 + y], x * dy + y, edges)
    pk1[0], pk1[1] = edges

    @pl.when(ix == 0)
    def _():
        zero(r1.at[0:dx])
        zero(ed1.at[:, 0])
        zero(r3.at[0])
        zero(ed3.at[:, 0])

    @pl.when(ix == nx - 1)
    def _():
        zero(r1.at[2 * dx : 3 * dx])
        zero(ed1.at[:, 2])
        zero(r3.at[dx + 1])
        zero(ed3.at[:, 2])

    @pl.when(iy == 0)
    def _():
        zero(r1.at[:, 0:3])
        zero(ed1.at[:, :, 0])

    @pl.when(iy == ny - 1)
    def _():
        zero(r1.at[:, 3 + dy : 6 + dy])
        zero(ed1.at[:, :, 2])

    @pl.when(iz == 0)
    def _():
        zero(ed1.at[0])
        zero(ed2.at[0])
        zero(ed3.at[0])

    @pl.when(iz == nz - 1)
    def _():
        zero(ed1.at[1])
        zero(ed2.at[1])
        zero(ed3.at[1])

    def span(index, count):
        return 3 - (index == 0).astype(jnp.int32) - (index == count - 1).astype(jnp.int32)

    near = span(ix, nx) * span(iy, ny) * span(iz, nz) - 1
    pl.semaphore_wait(barrier, near + nz - 1 + len(turns))

    def send_vol(n):
        (ox, oy, oz), far = VOLUME[n]
        if oz:
            src = pk1.at[1 if oz > 0 else 0]
            dst = ed1.at[0 if oz > 0 else 1, 1 - ox, 1 - oy]
        elif oy == 0:
            own = dx if (ox < 0) != far else 2 * dx - 1
            to = own - dx * ox
            src = r1.at[own, 3 : 3 + dy]
            dst = r1.at[to, 3 : 3 + dy]
        else:
            src_y = 3 if oy < 0 else dy
            dst_y = 0 if oy > 0 else 3 + dy
            to = dx * (1 - ox)
            src = r1.at[dx : 2 * dx, src_y : src_y + 3]
            dst = r1.at[to : to + dx, dst_y : dst_y + 3]
        return copy(src, dst, xs1.at[n], xr1.at[n], at(ox, oy, oz))

    def back(o):
        return there(*(-c for c in o))

    for n, (o, _) in enumerate(VOLUME):
        guarded(there(*o), lambda: send_vol(n).start())

    def take_vol(test):
        for n, (o, far) in enumerate(VOLUME):
            if test(o, far):
                guarded(back(o), lambda: send_vol(n).wait_recv())

    taps = w_first.shape[0]
    third = taps // 3
    w1t[0:chan, :] = w_first[...].T
    w1t[chan:two, :] = v_first[...].T
    for f, w_ref in enumerate((w_second, v_second)):
        turned = w_ref[...].T
        for kx in range(3):
            w2t[chan * (2 - kx) : chan * (3 - kx), third * f : third * (f + 1)] = turned[:, third * kx : third * (kx + 1)]
    for k in range(27):
        kx, rest = k // 9, k % 9
        w3t[chan * (2 - kx) : chan * (3 - kx), chan * rest : chan * (rest + 1)] = w_second[chan * (26 - k) : chan * (27 - k), :]
    for x in range(dx):
        zero(ej.at[x, 0:3])
        zero(ej.at[x, 3 + dy : 5 + dy])
        zero(eb.at[x, 0:3])
        zero(eb.at[x, 3 + dy : 5 + dy])

    def shift(raw_ref, out_ref, x, y, left, right, j):
        raw = raw_ref[x, y]
        before = left if j == 0 else pltpu.roll(left, 128 - j, 1)
        after = right if j == 127 else pltpu.roll(right, 127 - j, 1)
        out_ref[x, y, 0:chan] = jnp.where(lane == 0, before, pltpu.roll(raw, 1, 1))
        out_ref[x, y, chan:two] = jnp.where(lane == 127, after, pltpu.roll(raw, 127, 1))

    def slab1(planes, lines):
        for x in planes:
            for y in lines:
                bx, by = x // dx, (y + dy - 3) // dy
                shift(r1, q1, x, y, ed1[0, bx, by], ed1[1, bx, by], (x % dx) * dy + (y + dy - 3) % dy)

    def three(raw_ref, out_ref, x, y):
        return [out_ref[x, y, 0:chan], raw_ref[x, y], out_ref[x, y, chan:two]]

    def layer1(x, y, carry):
        halves = []
        for half in range(2):
            pieces = []
            for kx in range(3):
                for ky in range(3):
                    pieces += three(r1, q1, x + kx, y + half + ky)
            halves.append(jnp.concatenate(pieces, axis=0))
        both = jnp.dot(w1t[...], jnp.concatenate(halves, axis=1), preferred_element_type=F32)
        hidden, slope = gelu_pair(both[0:chan])
        gx_cell = ix * dx + x - 1
        gy_cell = iy * dy + y - 2
        inside = jnp.logical_and(
            jnp.logical_and(gx_cell >= 0, gx_cell < nx * dx), jnp.logical_and(gy_cell >= 0, gy_cell < ny * dy)
        )
        keep = inside.astype(F32)
        tangent = (keep * (slope * both[chan:two])).astype(BF16)
        hidden = (keep * hidden).astype(BF16)
        fields = [carry[0:2], carry[2:4]]
        for half in range(2):
            cols = slice(128 * half, 128 * half + 128)
            for f, value in enumerate((tangent, hidden)):
                r2[f, x, y + half] = value[:, cols]
                fields[f] = packed(value[:, cols], x * hy + y + half, fields[f])
            slope_ref[x, y + half] = slope[:, cols]
        return (*fields[0], *fields[1])

    own_y = range(3, 3 + dy)
    halo_y = [*range(3), *range(3 + dy, 6 + dy)]
    inner = (dy - 4) // 2
    take_vol(lambda o, far: o[0] == 0 and o[1] == 0)
    slab1(range(dx, 2 * dx), own_y)
    take_vol(lambda o, far: o[0] != 0 and o[1] == 0 and not far)
    slab1((dx - 1, 2 * dx), own_y)
    edges = lax.fori_loop(
        0, dx * inner, lambda i, c: layer1(1 + i // inner, 4 + 2 * lax.rem(i, inner), c), (blank,) * 4, unroll=4
    )
    take_vol(lambda o, far: far)
    slab1((0, 3 * dx - 1), own_y)
    edges = lax.fori_loop(
        0, 2 * inner, lambda i, c: layer1((hx - 1) * (i // inner), 4 + 2 * lax.rem(i, inner), c), edges, unroll=4
    )
    take_vol(lambda o, far: o[1] != 0)
    slab1(range(3 * dx), halo_y)

    def outer(i, c):
        k = lax.rem(i, 4)
        return layer1(i // 4, 2 * lax.rem(k, 2) + dy * (k // 2), c)

    edges = lax.fori_loop(0, hx * 4, outer, edges, unroll=4)
    pk2[0, 0], pk2[1, 0], pk2[0, 1], pk2[1, 1] = edges

    def send_hid(n, oz):
        return copy(pk2.at[n], ed2.at[1 - n], xs2.at[n], xr2.at[n], at(0, 0, oz))

    for n, oz in enumerate((-1, 1)):
        guarded(there(0, 0, oz), lambda: send_hid(n, oz).start())
    for n, oz in enumerate((-1, 1)):
        guarded(there(0, 0, -oz), lambda: send_hid(n, oz).wait_recv())

    for f in range(2):
        for x in range(hx):
            for y in range(hy):
                shift(r2.at[f], q2.at[f], x, y, ed2[0, f], ed2[1, f], x * hy + y)

    def layer2(pair, carry):
        y = 2 * pair
        out = [None] * dx
        for x in range(hx):
            halves = []
            for half in range(2):
                pieces = []
                for f in range(2):
                    for ky in range(3):
                        pieces += three(r2.at[f], q2.at[f], x, y + half + ky)
                halves.append(jnp.concatenate(pieces, axis=0))
            low, high = max(0, x - 2), min(dx - 1, x)
            left = w2t[chan * (2 - x + low) : chan * (3 - x + high), :]
            product = jnp.dot(left, jnp.concatenate(halves, axis=1), preferred_element_type=F32)
            for to in range(low, high + 1):
                term = product[chan * (to - low) : chan * (to - low + 1)]
                out[to] = term if out[to] is None else out[to] + term
        for x in range(dx):
            for half in range(2):
                gy_cell = iy * dy + y + half - 1
                keep = jnp.logical_and(gy_cell >= 0, gy_cell < ny * dy).astype(F32)
                value = (keep * out[x][:, 128 * half : 128 * half + 128]).astype(BF16)
                r3[x + 1, y + half] = value
                carry = packed(value, x * (dy + 2) + y + half, carry)
        return carry

    cut = 2 * ((dy + 2 + 2) // 4)

    def send_plane(n, ox, late):
        lines = slice(cut, dy + 2) if late else slice(0, cut)
        return copy(
            r3.at[1 if ox < 0 else dx, lines], r3.at[dx + 1 if ox < 0 else 0, lines],
            ps3.at[n, int(late)], pr3.at[n, int(late)], at(ox, 0, 0),
        )

    def send_jv(n):
        ox, oz = SIDES[n]
        return copy(pk3.at[1 if oz > 0 else 0], ed3.at[0 if oz > 0 else 1, 1 - ox], xs3.at[n], xr3.at[n], at(ox, 0, oz))

    edges = lax.fori_loop(0, cut // 2, layer2, (blank, blank), unroll=cut // 2)
    for n, ox in enumerate((-1, 1)):
        guarded(there(ox, 0, 0), lambda: send_plane(n, ox, False).start())
    rest = (dy + 2 - cut) // 2
    pk3[0], pk3[1] = lax.fori_loop(0, rest, lambda i, c: layer2(cut // 2 + i, c), edges, unroll=rest)
    for n, (ox, oz) in enumerate(SIDES):
        guarded(there(ox, 0, oz), lambda: send_jv(n).start())
    for n, ox in enumerate((-1, 1)):
        guarded(there(ox, 0, 0), lambda: send_plane(n, ox, True).start())

    for x in range(dx):
        own = r3[x + 1, 1 : 1 + dy]
        ej[x, 3 : 3 + dy] = own
        jv_out[x] = own

    def correlate(raw_ref, out_ref, x0, y0, e_ref):
        total = None
        for x in range(dx):
            lhs, rhs = [], []
            for q in range(dy + 2):
                pieces = []
                for kx in range(3):
                    pieces += three(raw_ref, out_ref, x + kx + x0, q + y0)
                lhs.append(jnp.concatenate(pieces, axis=0))
                rhs.append(jnp.concatenate([e_ref[x, q - ky + 3] for ky in range(4)], axis=0))
            product = lax.dot_general(
                jnp.concatenate(lhs, axis=1), jnp.concatenate(rhs, axis=1),
                (((1,), (1,)), ((), ())), preferred_element_type=F32,
            )
            total = product if total is None else total + product
        return total

    lane8 = lax.broadcasted_iota(jnp.int32, (8, 128), 1)

    def put_part(f, value):
        for t in range(nz * tiles):
            if t < 27:
                j, s = t // 9, t % 9
                tail = pltpu.roll(value[216 + 8 * s : 224 + 8 * s], 96 - 32 * j, 1)
                part[t // tiles, f, t % tiles] = jnp.where(lane8 < 96, value[8 * t : 8 * t + 8], tail)
            else:
                part[t // tiles, f, t % tiles] = jnp.zeros((8, 128), F32)

    def send1(f, d):
        return copy(part.at[zs[d], f], recv1.at[d - 1, f], as1.at[f, d - 1], ar1.at[f, d - 1], z_peer(d))

    put_part(0, correlate(r2.at[1], q2.at[1], 0, 1, ej))
    for d in range(1, nz):
        send1(0, d).start()

    def take_jv(own):
        for n, (ox, oz) in enumerate(SIDES):
            if (ox == 0) == own:
                guarded(there(-ox, 0, -oz), lambda: send_jv(n).wait_recv())

    def slab3(planes):
        for x in planes:
            bx = (x + dx - 1) // dx
            for y in range(dy + 2):
                shift(r3, q3, x, y, ed3[0, bx], ed3[1, bx], ((x + dx - 1) % dx) * (dy + 2) + y)

    def layer3(x, y):
        halves = []
        for half in range(2):
            pieces = []
            for ky in range(3):
                pieces += three(r3, q3, x, y + half + ky)
            halves.append(jnp.concatenate(pieces, axis=0))
        low, high = max(0, x - 2), min(dx - 1, x)
        left = w3t[chan * (2 - x + low) : chan * (3 - x + high), :]
        product = jnp.dot(left, jnp.concatenate(halves, axis=1), preferred_element_type=F32)
        return {to: product[chan * (to - low) : chan * (to - low + 1)] for to in range(low, high + 1)}

    take_jv(True)
    slab3(range(1, dx + 1))

    def own3(pair, _):
        y = 2 * pair
        parts = [layer3(x, y) for x in range(1, dx + 1)]
        for x in range(dx):
            summed = parts[0][x] + parts[1][x]
            for half in range(2):
                acc3[x, y + half] = summed[:, 128 * half : 128 * half + 128]
        return 0

    lax.fori_loop(0, dy // 2, own3, 0, unroll=4)
    take_jv(False)
    for n, ox in enumerate((-1, 1)):
        for late in (False, True):
            guarded(there(-ox, 0, 0), lambda: send_plane(n, ox, late).wait_recv())
    slab3((0, dx + 1))

    def halo3(pair, _):
        y = 2 * pair
        for x, plane_x in ((0, 0), (dx - 1, dx + 1)):
            term = layer3(plane_x, y)[x]
            for half in range(2):
                cols = slice(128 * half, 128 * half + 128)
                value = slope_ref[x + 1, y + half + 2] * (acc3[x, y + half] + term[:, cols])
                eb[x, y + half + 3] = value.astype(BF16)
        return 0

    lax.fori_loop(0, dy // 2, halo3, 0, unroll=4)

    put_part(1, correlate(r1, q1, 1, 2, eb))
    for d in range(1, nz):
        send1(1, d).start()

    for f in range(2):
        total = part[iz, f]
        for d in range(1, nz):
            send1(f, d).wait_recv()
            total = total + recv1[d - 1, f]
        for r in range(nx * ny * share):
            slot = slice(f * share + r % share, f * share + r % share + 1)
            if r < 8 * tiles:
                rows[r // share, slot, :] = total[r // 8, r % 8 : r % 8 + 1, :]
            else:
                rows[r // share, slot, :] = jnp.zeros((1, 128), F32)

    def send2(n):
        ey, ex = turns[n]
        return copy(rows.at[ys[ey] * nx + xs[ex]], recv2.at[n], as2.at[n], ar2.at[n], p_peer(n))

    def send3(n):
        return copy(gath.at[me], gath.at[me], as3.at[n], ar3.at[n], p_peer(n))

    for n in range(len(turns)):
        send2(n).start()
    total = rows[me]
    for n in range(len(turns)):
        send2(n).wait_recv()
        total = total + recv2[n]
    gath[me] = total
    for n in range(len(turns)):
        send3(n).start()
    for n in range(len(turns)):
        send3(n).wait_recv()
    for f in range(2):
        for r in range(8 * tiles):
            slot = slice(f * share + r % share, f * share + r % share + 1)
            chunk[f, r // 8, r % 8 : r % 8 + 1, :] = gath[r // share, slot, :]

    def send4(d):
        return copy(chunk, tot.at[iz], as4.at[d - 1], ar4.at[d - 1], z_peer(d))

    for d in range(1, nz):
        send4(d).start()
    tot[iz] = chunk[...]
    for d in range(1, nz):
        send4(d).wait_recv()

    for n, (o, _) in enumerate(VOLUME):
        guarded(there(*o), lambda: send_vol(n).wait_send())
    for n, oz in enumerate((-1, 1)):
        guarded(there(0, 0, oz), lambda: send_hid(n, oz).wait_send())
    for n, ox in enumerate((-1, 1)):
        for late in (False, True):
            guarded(there(ox, 0, 0), lambda: send_plane(n, ox, late).wait_send())
    for n, (ox, oz) in enumerate(SIDES):
        guarded(there(ox, 0, oz), lambda: send_jv(n).wait_send())
    for d in range(1, nz):
        send1(0, d).wait_send()
        send1(1, d).wait_send()
        send4(d).wait_send()
    for n in range(len(turns)):
        send2(n).wait_send()
        send3(n).wait_send()


def last_kernel(tiles, count_all, factor, tot, jv_raw, v_first, v_second, jv, gv_first, gv_second):
    for x in range(jv_raw.shape[0]):
        jv[:, x] = jnp.transpose(jv_raw[x], (1, 0, 2))
    for f, (v_ref, out) in enumerate(((v_second, gv_second), (v_first, gv_first))):
        tile = [tot[t // tiles, f, t % tiles] for t in range(27)]
        for kx in range(3):
            for ky in range(3):
                pieces = []
                for u in range(12 * kx, 12 * kx + 12):
                    if u < 27:
                        piece = tile[u] if ky == 0 else pltpu.roll(tile[u], 128 - 32 * ky, 1)
                    else:
                        piece = pltpu.roll(tile[9 * ky + u - 27], 32, 1)
                    pieces.append(piece[:, 0:32])
                k = 3 * kx + ky
                summed = jnp.concatenate(pieces, axis=0)
                base = v_ref[96 * k : 96 * k + 96, :].astype(F32)
                out[k] = factor * (summed / count_all + 0.1 * base)


def body(volume, w_first, w_second, v_first, v_second):
    chan, dx, dy, dz = volume.shape
    nx, ny, nz = lax.axis_size("gx"), lax.axis_size("gy"), lax.axis_size("gz")
    plane = nx * ny
    tiles = -(-27 // nz)
    share = -(-8 * tiles // plane)
    count_all = float(dx * dy * dz * nx * ny * nz)
    factor = math.sqrt(27.0 * chan)
    shape = w_first.shape
    flat = [w.reshape(27 * chan, chan) for w in (w_first, w_second, v_first, v_second)]
    vm = pl.BlockSpec(memory_space=pltpu.VMEM)
    dma = pltpu.SemaphoreType.DMA
    tot, jv_raw = pl.pallas_call(
        functools.partial(main_kernel, nx, ny, nz, dx, dy, tiles, share),
        out_shape=(
            jax.ShapeDtypeStruct((nz, 2, tiles, 8, 128), F32),
            jax.ShapeDtypeStruct((dx, dy, chan, 128), BF16),
        ),
        in_specs=[vm] * 5,
        out_specs=(vm, vm),
        scratch_shapes=[
            pltpu.VMEM((3 * dx, dy + 6, chan, 128), BF16),
            pltpu.VMEM((3 * dx, dy + 6, 2 * chan, 128), BF16),
            pltpu.VMEM((2, dx + 2, dy + 4, chan, 128), BF16),
            pltpu.VMEM((2, dx + 2, dy + 4, 2 * chan, 128), BF16),
            pltpu.VMEM((dx + 2, dy + 2, chan, 128), BF16),
            pltpu.VMEM((dx + 2, dy + 2, 2 * chan, 128), BF16),
            pltpu.VMEM((dx + 2, dy + 4, chan, 128), F32),
            pltpu.VMEM((dx, dy, chan, 128), F32),
            pltpu.VMEM((dx, dy + 5, chan, 128), BF16),
            pltpu.VMEM((dx, dy + 5, chan, 128), BF16),
            pltpu.VMEM((2 * chan, 27 * chan), BF16),
            pltpu.VMEM((3 * chan, 18 * chan), BF16),
            pltpu.VMEM((3 * chan, 9 * chan), BF16),
            pltpu.VMEM((2, chan, 128), BF16),
            pltpu.VMEM((2, 3, 3, chan, 128), BF16),
            pltpu.VMEM((2, 2, chan, 128), BF16),
            pltpu.VMEM((2, 2, chan, 128), BF16),
            pltpu.VMEM((2, chan, 128), BF16),
            pltpu.VMEM((2, 3, chan, 128), BF16),
            pltpu.VMEM((nz, 2, tiles, 8, 128), F32),
            pltpu.VMEM((nz - 1, 2, tiles, 8, 128), F32),
            pltpu.VMEM((plane, 2 * share, 128), F32),
            pltpu.VMEM((plane - 1, 2 * share, 128), F32),
            pltpu.VMEM((plane, 2 * share, 128), F32),
            pltpu.VMEM((2, tiles, 8, 128), F32),
            dma((len(VOLUME),)), dma((len(VOLUME),)),
            dma((2,)), dma((2,)),
            dma((6,)), dma((6,)),
            dma((2, 2)), dma((2, 2)),
            dma((2, nz - 1)), dma((2, nz - 1)),
            dma((plane - 1,)), dma((plane - 1,)),
            dma((plane - 1,)), dma((plane - 1,)),
            dma((nz - 1,)), dma((nz - 1,)),
        ],
        compiler_params=pltpu.CompilerParams(collective_id=0, has_side_effects=True),
        cost_estimate=pl.CostEstimate(flops=2000000000, bytes_accessed=2000000, transcendentals=400000),
    )(volume, *flat)
    jv, gv_first, gv_second = pl.pallas_call(
        functools.partial(last_kernel, tiles, count_all, factor),
        out_shape=(
            jax.ShapeDtypeStruct((chan, dx, dy, 128), BF16),
            jax.ShapeDtypeStruct((9, 3 * chan, chan), F32),
            jax.ShapeDtypeStruct((9, 3 * chan, chan), F32),
        ),
        in_specs=[vm] * 4,
        out_specs=(vm, vm, vm),
    )(tot, jv_raw, flat[2], flat[3])
    return (jv, gv_first.reshape(shape), gv_second.reshape(shape))


def solution(mesh):
    in_specs = (P(None, "gx", "gy", "gz"), P(), P(), P(), P())
    out_specs = (P(None, "gx", "gy", "gz"), P(), P())
    return jax.shard_map(body, mesh=mesh, in_specs=in_specs, out_specs=out_specs, check_vma=False)
```

time: 102 us -> 68.7 us (0.67)
  Pallas kernels: 102 us -> 67.9 us
    pallas_call x1, Pallas kernels: 99.2 us -> 65.5 us  [body(): pl.pallas_call(functools.partial(main_kernel, nx, ny, nz, dx, dy, tiles,...]
where the time goes in v3:
time: 68.7 us; the launch traced here: 68.6 us
  Pallas kernels  67.9 us (99%)
    pallas_call x1, Pallas kernels, body(): pl.pallas_call(functools.partial(main_kernel, nx, ny, nz, dx, dy, tiles,...  65.5 us
    pallas_call x1, Pallas kernels, body(): pl.pallas_call(functools.partial(last_kernel, tiles, count_all, factor),...  2.41 us

profile of v3, /device:TPU:1, one launch (start us, length us, event | category | flops | bytes accessed | tf_op | source)
XLA Modules:
  0.0 68.6 jit_solution(6020219149615202638)
XLA Ops:
  0.6 65.5 %shard_map.76 = (f32[8,2,4,8,128]{4,3,2,1,0:T(8,128)}, bf16[2,16,32,128]{3,2,1,0:T(8,128)(2,1)}) custom-call(bf16[32,2,16,128]{3,2,1,0:T(8,128)(2,1)} %vol.1, bf16[864,32]{1,0:T(8,128)(2,1)} %bitcast.12, bf16[864,32]{1,0:T(8,128)(2,1)} %bitcast.13, bf16[864,32]{1,0:T(8,128)(2,1)} %bitcast.6, bf16[864,32]{1,0:T(8,128)(2,1)} %bitcast.8), custom_call_target="tpu_custom_call" | custom-call | flops 2000000000 | bytes 2000000 | tf_op jit(solution)/shard_map/pallas_call | solution.py:520
  66.2 2.4 %shard_map.77 = (bf16[32,2,16,128]{3,2,1,0:T(8,128)(2,1)}, f32[9,96,32]{2,1,0:T(8,128)}, f32[9,96,32]{2,1,0:T(8,128)}) custom-call(f32[8,2,4,8,128]{4,3,2,1,0:T(8,128)} %get-tuple-element.8.tot, bf16[2,16,32,128]{3,2,1,0:T(8,128)(2,1)} %get-tuple-element.9.jv_raw, bf16[864,32]{1,0:T(8,128)(2,1)} %bitcast.7, bf16[864,32]{1,0:T(8,128)(2,1)} %bitcast.9), custom_call_target="tpu_custom_call" | custom-call | tf_op jit(solution)/shard_map/pallas_call | solution.py:566

commit v4 on v3

--- a/solution.py
+++ b/solution.py
@@ -13,9 +13,10 @@
 BF16 = jnp.bfloat16
 F32 = jnp.float32
 OFFSETS = [o for o in itertools.product((-1, 0, 1), repeat=3) if o != (0, 0, 0)]
-VOLUME = [((ox, 0, 0), False) for ox in (-1, 1)]
+VOLUME = [(o, False) for o in OFFSETS if o[1] != 0 and o[2] == 0]
+VOLUME += [(o, False) for o in OFFSETS if o[1] != 0 and o[2] != 0]
+VOLUME += [((ox, 0, 0), False) for ox in (-1, 1)]
 VOLUME += [((ox, 0, oz), False) for ox in (0, -1, 1) for oz in (-1, 1)]
-VOLUME += [(o, False) for o in OFFSETS if o[1] != 0]
 VOLUME += [((ox, 0, 0), True) for ox in (-1, 1)]
 SIDES = [(ox, oz) for ox in (-1, 0, 1) for oz in (-1, 1)]
 
@@ -30,14 +31,14 @@
 
 
 def main_kernel(
-    nx, ny, nz, dx, dy, tiles, share,
-    vol, w_first, w_second, v_first, v_second,
+    nx, ny, nz, dx, dy,
+    vol_in, w_first_in, w_second_in, v_first_in, v_second_in,
     tot, jv_out,
-    r1, q1, r2, q2, r3, q3, slope_ref, acc3, ej, eb, w1t, w2t, w3t,
+    vol, w_first, w_second, v_first, v_second, load, r1, q1, r2, q2, r3, q3, slope_ref, acc3, ej, eb, w1t, w2t, w3t,
     pk1, ed1, pk2, ed2, pk3, ed3,
-    part, recv1, rows, recv2, gath, chunk,
+    part, recv_a, sum_a, recv_z, fin,
     xs1, xr1, xs2, xr2, xs3, xr3, ps3, pr3,
-    as1, ar1, as2, ar2, as3, ar3, as4, ar4,
+    sa, ra, sz, rz, sg, rg,
 ):
     ix, iy, iz = lax.axis_index("gx"), lax.axis_index("gy"), lax.axis_index("gz")
     me = iy * nx + ix
@@ -57,17 +58,23 @@
     def at(ox, oy, oz):
         return {"gx": ix + ox, "gy": iy + oy, "gz": iz + oz}
 
+    wide = 4
+    high = ny // wide
+    planes = high * nx
+    col, row = lax.rem(iy, wide), iy // wide
+    level = row * nx + ix
     zs = [lax.rem(iz + d, nz) for d in range(nz)]
-    ys = [lax.rem(iy + d, ny) for d in range(ny)]
-    xs = [lax.rem(ix + d, nx) for d in range(nx)]
-    turns = [(ey, ex) for ey in range(ny) for ex in range(nx)][1:]
+    cs = [lax.rem(col + d, wide) for d in range(wide)]
+    turns = [(ez, ec) for ez in range(nz) for ec in range(wide)][1:]
+    me = iz * wide + col
+
+    def a_peer(n):
+        ez, ec = turns[n]
+        return {"gx": ix, "gy": row * wide + cs[ec], "gz": zs[ez]}
 
     def z_peer(d):
-        return {"gx": ix, "gy": iy, "gz": zs[d]}
-
-    def p_peer(n):
-        ey, ex = turns[n]
-        return {"gx": xs[ex], "gy": ys[ey], "gz": iz}
+        other = lax.rem(level + d, planes)
+        return {"gx": lax.rem(other, nx), "gy": (other // nx) * wide + col, "gz": iz}
 
     def copy(src, dst, send, recv, peer):
         return pltpu.make_async_remote_copy(src, dst, send, recv, device_id=peer, device_id_type=MESH)
@@ -77,21 +84,30 @@
         def _():
             action()
 
+    loads = [
+        pltpu.make_async_copy(src, dst, load.at[n])
+        for n, (src, dst) in enumerate(
+            ((vol_in, vol), (w_first_in, w_first), (w_second_in, w_second), (v_first_in, v_first), (v_second_in, v_second))
+        )
+    ]
+    for step in loads:
+        step.start()
     barrier = pltpu.get_barrier_semaphore()
 
     def greet(peer):
         pl.semaphore_signal(barrier, inc=1, device_id=peer, device_id_type=MESH)
 
+    for d in range(1, planes):
+        greet(z_peer(d))
     for n in range(len(turns)):
-        greet(p_peer(n))
+        greet(a_peer(n))
     for o in OFFSETS:
         guarded(there(*o), lambda: greet(at(*o)))
-    for d in range(1, nz):
-        greet(z_peer(d))
 
     def zero(ref):
         ref[...] = jnp.zeros(ref.shape, ref.dtype)
 
+    loads[0].wait()
     for x in range(dx):
         r1[dx + x, 3 : 3 + dy] = jnp.transpose(vol[:, x], (1, 0, 2))
 
@@ -147,7 +163,7 @@
         return 3 - (index == 0).astype(jnp.int32) - (index == count - 1).astype(jnp.int32)
 
     near = span(ix, nx) * span(iy, ny) * span(iz, nz) - 1
-    pl.semaphore_wait(barrier, near + nz - 1 + len(turns))
+    pl.semaphore_wait(barrier, near + planes - 1 + len(turns))
 
     def send_vol(n):
         (ox, oy, oz), far = VOLUME[n]
@@ -178,6 +194,8 @@
             if test(o, far):
                 guarded(back(o), lambda: send_vol(n).wait_recv())
 
+    for step in loads[1:]:
+        step.wait()
     taps = w_first.shape[0]
     third = taps // 3
     w1t[0:chan, :] = w_first[...].T
@@ -202,11 +220,26 @@
         out_ref[x, y, 0:chan] = jnp.where(lane == 0, before, pltpu.roll(raw, 1, 1))
         out_ref[x, y, chan:two] = jnp.where(lane == 127, after, pltpu.roll(raw, 127, 1))
 
-    def slab1(planes, lines):
-        for x in planes:
+    def turn(raw_ref, out_ref, x, y):
+        raw = raw_ref[x, y]
+        out_ref[x, y, 0:chan] = pltpu.roll(raw, 1, 1)
+        out_ref[x, y, chan:two] = pltpu.roll(raw, 127, 1)
+
+    def patch(out_ref, x, y, left, right, j):
+        before = left if j == 0 else pltpu.roll(left, 128 - j, 1)
+        after = right if j == 127 else pltpu.roll(right, 127 - j, 1)
+        out_ref[x, y, 0:chan] = jnp.where(lane == 0, before, out_ref[x, y, 0:chan])
+        out_ref[x, y, chan:two] = jnp.where(lane == 127, after, out_ref[x, y, chan:two])
+
+    def slab1(which, lines, turned=False):
+        for x in which:
             for y in lines:
                 bx, by = x // dx, (y + dy - 3) // dy
-                shift(r1, q1, x, y, ed1[0, bx, by], ed1[1, bx, by], (x % dx) * dy + (y + dy - 3) % dy)
+                place = (ed1[0, bx, by], ed1[1, bx, by], (x % dx) * dy + (y + dy - 3) % dy)
+                if turned:
+                    patch(q1, x, y, *place)
+                else:
+                    shift(r1, q1, x, y, *place)
 
     def three(raw_ref, out_ref, x, y):
         return [out_ref[x, y, 0:chan], raw_ref[x, y], out_ref[x, y, chan:two]]
@@ -241,26 +274,30 @@
     own_y = range(3, 3 + dy)
     halo_y = [*range(3), *range(3 + dy, 6 + dy)]
     inner = (dy - 4) // 2
+    for x in range(dx, 2 * dx):
+        for y in own_y:
+            turn(r1, q1, x, y)
     take_vol(lambda o, far: o[0] == 0 and o[1] == 0)
-    slab1(range(dx, 2 * dx), own_y)
+    slab1(range(dx, 2 * dx), own_y, True)
     take_vol(lambda o, far: o[0] != 0 and o[1] == 0 and not far)
     slab1((dx - 1, 2 * dx), own_y)
     edges = lax.fori_loop(
-        0, dx * inner, lambda i, c: layer1(1 + i // inner, 4 + 2 * lax.rem(i, inner), c), (blank,) * 4, unroll=4
-    )
-    take_vol(lambda o, far: far)
-    slab1((0, 3 * dx - 1), own_y)
-    edges = lax.fori_loop(
-        0, 2 * inner, lambda i, c: layer1((hx - 1) * (i // inner), 4 + 2 * lax.rem(i, inner), c), edges, unroll=4
+        0, dx * inner, lambda i, c: layer1(1 + i // inner, 4 + 2 * lax.rem(i, inner), c), (blank,) * 4, unroll=6
     )
     take_vol(lambda o, far: o[1] != 0)
-    slab1(range(3 * dx), halo_y)
+    slab1(range(1, 3 * dx - 1), halo_y)
 
     def outer(i, c):
         k = lax.rem(i, 4)
-        return layer1(i // 4, 2 * lax.rem(k, 2) + dy * (k // 2), c)
-
-    edges = lax.fori_loop(0, hx * 4, outer, edges, unroll=4)
+        return layer1(1 + i // 4, 2 * lax.rem(k, 2) + dy * (k // 2), c)
+
+    edges = lax.fori_loop(0, dx * 4, outer, edges, unroll=8)
+    take_vol(lambda o, far: far)
+    slab1((0, 3 * dx - 1), range(dy + 6))
+    pairs = hy // 2
+    edges = lax.fori_loop(
+        0, 2 * pairs, lambda i, c: layer1((hx - 1) * (i // pairs), 2 * lax.rem(i, pairs), c), edges, unroll=10
+    )
     pk2[0, 0], pk2[1, 0], pk2[0, 1], pk2[1, 1] = edges
 
     def send_hid(n, oz):
@@ -268,13 +305,17 @@
 
     for n, oz in enumerate((-1, 1)):
         guarded(there(0, 0, oz), lambda: send_hid(n, oz).start())
-    for n, oz in enumerate((-1, 1)):
-        guarded(there(0, 0, -oz), lambda: send_hid(n, oz).wait_recv())
-
     for f in range(2):
         for x in range(hx):
             for y in range(hy):
-                shift(r2.at[f], q2.at[f], x, y, ed2[0, f], ed2[1, f], x * hy + y)
+                turn(r2.at[f], q2.at[f], x, y)
+    for n, oz in enumerate((-1, 1)):
+        guarded(there(0, 0, -oz), lambda: send_hid(n, oz).wait_recv())
+
+    for f in range(2):
+        for x in range(hx):
+            for y in range(hy):
+                patch(q2.at[f], x, y, ed2[0, f], ed2[1, f], x * hy + y)
 
     def layer2(pair, carry):
         y = 2 * pair
@@ -328,7 +369,6 @@
     for x in range(dx):
         own = r3[x + 1, 1 : 1 + dy]
         ej[x, 3 : 3 + dy] = own
-        jv_out[x] = own
 
     def correlate(raw_ref, out_ref, x0, y0, e_ref):
         total = None
@@ -350,31 +390,68 @@
     lane8 = lax.broadcasted_iota(jnp.int32, (8, 128), 1)
 
     def put_part(f, value):
-        for t in range(nz * tiles):
+        for t in range(nz * wide):
             if t < 27:
                 j, s = t // 9, t % 9
                 tail = pltpu.roll(value[216 + 8 * s : 224 + 8 * s], 96 - 32 * j, 1)
-                part[t // tiles, f, t % tiles] = jnp.where(lane8 < 96, value[8 * t : 8 * t + 8], tail)
+                part[t, f] = jnp.where(lane8 < 96, value[8 * t : 8 * t + 8], tail)
             else:
-                part[t // tiles, f, t % tiles] = jnp.zeros((8, 128), F32)
-
-    def send1(f, d):
-        return copy(part.at[zs[d], f], recv1.at[d - 1, f], as1.at[f, d - 1], ar1.at[f, d - 1], z_peer(d))
-
-    put_part(0, correlate(r2.at[1], q2.at[1], 0, 1, ej))
-    for d in range(1, nz):
-        send1(0, d).start()
+                part[t, f] = jnp.zeros((8, 128), F32)
+
+    def send_a(f, n):
+        ez, ec = turns[n]
+        return copy(part.at[zs[ez] * wide + cs[ec], f], recv_a.at[f, n], sa.at[f], ra.at[f], a_peer(n))
+
+    def send_z(f, d):
+        return copy(sum_a.at[f], recv_z.at[f, level], sz.at[f], rz.at[f], z_peer(d))
+
+    def send_g(f, n):
+        return copy(fin.at[f], tot.at[me, f], sg.at[f], rg.at[f], a_peer(n))
+
+    def settle(ref, sem):
+        pltpu.make_async_copy(ref, ref, sem).wait()
+
+    def start_a(f, value):
+        put_part(f, value)
+        for n in range(len(turns)):
+            send_a(f, n).start()
+
+    def start_z(f):
+        settle(recv_a.at[f], ra.at[f])
+        total = part[me, f]
+        for n in range(len(turns)):
+            total = total + recv_a[f, n]
+        sum_a[f] = total
+        for d in range(1, planes):
+            send_z(f, d).start()
+        recv_z[f, level] = total
+
+    def start_g(f):
+        settle(recv_z.at[f, 1:planes], rz.at[f])
+        total = recv_z[f, 0]
+        for d in range(1, planes):
+            total = total + recv_z[f, d]
+        fin[f] = total
+        for n in range(len(turns)):
+            send_g(f, n).start()
+        tot[me, f] = total
+
+    start_a(0, correlate(r2.at[1], q2.at[1], 0, 1, ej))
 
     def take_jv(own):
         for n, (ox, oz) in enumerate(SIDES):
             if (ox == 0) == own:
                 guarded(there(-ox, 0, -oz), lambda: send_jv(n).wait_recv())
 
-    def slab3(planes):
-        for x in planes:
+    def slab3(which, turned=False):
+        for x in which:
             bx = (x + dx - 1) // dx
             for y in range(dy + 2):
-                shift(r3, q3, x, y, ed3[0, bx], ed3[1, bx], ((x + dx - 1) % dx) * (dy + 2) + y)
+                place = (ed3[0, bx], ed3[1, bx], ((x + dx - 1) % dx) * (dy + 2) + y)
+                if turned:
+                    patch(q3, x, y, *place)
+                else:
+                    shift(r3, q3, x, y, *place)
 
     def layer3(x, y):
         halves = []
@@ -388,8 +465,11 @@
         product = jnp.dot(left, jnp.concatenate(halves, axis=1), preferred_element_type=F32)
         return {to: product[chan * (to - low) : chan * (to - low + 1)] for to in range(low, high + 1)}
 
+    for x in range(1, dx + 1):
+        for y in range(dy + 2):
+            turn(r3, q3, x, y)
     take_jv(True)
-    slab3(range(1, dx + 1))
+    slab3(range(1, dx + 1), True)
 
     def own3(pair, _):
         y = 2 * pair
@@ -419,53 +499,15 @@
 
     lax.fori_loop(0, dy // 2, halo3, 0, unroll=4)
 
-    put_part(1, correlate(r1, q1, 1, 2, eb))
-    for d in range(1, nz):
-        send1(1, d).start()
-
+    start_z(0)
+    start_a(1, correlate(r1, q1, 1, 2, eb))
+    for x in range(dx):
+        jv_out[:, x] = jnp.transpose(r3[x + 1, 1 : 1 + dy], (1, 0, 2))
+    start_g(0)
+    start_z(1)
+    start_g(1)
     for f in range(2):
-        total = part[iz, f]
-        for d in range(1, nz):
-            send1(f, d).wait_recv()
-            total = total + recv1[d - 1, f]
-        for r in range(nx * ny * share):
-            slot = slice(f * share + r % share, f * share + r % share + 1)
-            if r < 8 * tiles:
-                rows[r // share, slot, :] = total[r // 8, r % 8 : r % 8 + 1, :]
-            else:
-                rows[r // share, slot, :] = jnp.zeros((1, 128), F32)
-
-    def send2(n):
-        ey, ex = turns[n]
-        return copy(rows.at[ys[ey] * nx + xs[ex]], recv2.at[n], as2.at[n], ar2.at[n], p_peer(n))
-
-    def send3(n):
-        return copy(gath.at[me], gath.at[me], as3.at[n], ar3.at[n], p_peer(n))
-
-    for n in range(len(turns)):
-        send2(n).start()
-    total = rows[me]
-    for n in range(len(turns)):
-        send2(n).wait_recv()
-        total = total + recv2[n]
-    gath[me] = total
-    for n in range(len(turns)):
-        send3(n).start()
-    for n in range(len(turns)):
-        send3(n).wait_recv()
-    for f in range(2):
-        for r in range(8 * tiles):
-            slot = slice(f * share + r % share, f * share + r % share + 1)
-            chunk[f, r // 8, r % 8 : r % 8 + 1, :] = gath[r // share, slot, :]
-
-    def send4(d):
-        return copy(chunk, tot.at[iz], as4.at[d - 1], ar4.at[d - 1], z_peer(d))
-
-    for d in range(1, nz):
-        send4(d).start()
-    tot[iz] = chunk[...]
-    for d in range(1, nz):
-        send4(d).wait_recv()
+        settle(recv_a.at[f], rg.at[f])
 
     for n, (o, _) in enumerate(VOLUME):
         guarded(there(*o), lambda: send_vol(n).wait_send())
@@ -476,20 +518,16 @@
             guarded(there(ox, 0, 0), lambda: send_plane(n, ox, late).wait_send())
     for n, (ox, oz) in enumerate(SIDES):
         guarded(there(ox, 0, oz), lambda: send_jv(n).wait_send())
-    for d in range(1, nz):
-        send1(0, d).wait_send()
-        send1(1, d).wait_send()
-        send4(d).wait_send()
-    for n in range(len(turns)):
-        send2(n).wait_send()
-        send3(n).wait_send()
-
-
-def last_kernel(tiles, count_all, factor, tot, jv_raw, v_first, v_second, jv, gv_first, gv_second):
-    for x in range(jv_raw.shape[0]):
-        jv[:, x] = jnp.transpose(jv_raw[x], (1, 0, 2))
+    for f in range(2):
+        settle(recv_a.at[f], sa.at[f])
+        settle(recv_a.at[f], sg.at[f])
+        settle(recv_z.at[f, 1:planes], sz.at[f])
+
+
+def last_kernel(count_all, factor, tot, jv_in, v_first, v_second, jv, gv_first, gv_second):
+    jv[...] = jv_in[...]
     for f, (v_ref, out) in enumerate(((v_second, gv_second), (v_first, gv_first))):
-        tile = [tot[t // tiles, f, t % tiles] for t in range(27)]
+        tile = [tot[t, f] for t in range(27)]
         for kx in range(3):
             for ky in range(3):
                 pieces = []
@@ -508,24 +546,28 @@
 def body(volume, w_first, w_second, v_first, v_second):
     chan, dx, dy, dz = volume.shape
     nx, ny, nz = lax.axis_size("gx"), lax.axis_size("gy"), lax.axis_size("gz")
-    plane = nx * ny
-    tiles = -(-27 // nz)
-    share = -(-8 * tiles // plane)
+    group = 4 * nz
+    planes = nx * ny // 4
     count_all = float(dx * dy * dz * nx * ny * nz)
     factor = math.sqrt(27.0 * chan)
     shape = w_first.shape
     flat = [w.reshape(27 * chan, chan) for w in (w_first, w_second, v_first, v_second)]
     vm = pl.BlockSpec(memory_space=pltpu.VMEM)
+    far = functools.partial(pltpu.with_memory_space_constraint, memory_space=pltpu.HBM)
+    near = functools.partial(pltpu.with_memory_space_constraint, memory_space=pltpu.VMEM)
     dma = pltpu.SemaphoreType.DMA
-    tot, jv_raw = pl.pallas_call(
-        functools.partial(main_kernel, nx, ny, nz, dx, dy, tiles, share),
+    tot, jv_made = pl.pallas_call(
+        functools.partial(main_kernel, nx, ny, nz, dx, dy),
         out_shape=(
-            jax.ShapeDtypeStruct((nz, 2, tiles, 8, 128), F32),
-            jax.ShapeDtypeStruct((dx, dy, chan, 128), BF16),
+            pltpu.VMEM((group, 2, 8, 128), F32),
+            pltpu.VMEM((chan, dx, dy, 128), BF16),
         ),
-        in_specs=[vm] * 5,
+        in_specs=[pl.BlockSpec(memory_space=pltpu.HBM)] * 5,
         out_specs=(vm, vm),
         scratch_shapes=[
+            pltpu.VMEM(volume.shape, BF16),
+            *[pltpu.VMEM(flat[0].shape, BF16)] * 4,
+            dma((5,)),
             pltpu.VMEM((3 * dx, dy + 6, chan, 128), BF16),
             pltpu.VMEM((3 * dx, dy + 6, 2 * chan, 128), BF16),
             pltpu.VMEM((2, dx + 2, dy + 4, chan, 128), BF16),
@@ -545,34 +587,31 @@
             pltpu.VMEM((2, 2, chan, 128), BF16),
             pltpu.VMEM((2, chan, 128), BF16),
             pltpu.VMEM((2, 3, chan, 128), BF16),
-            pltpu.VMEM((nz, 2, tiles, 8, 128), F32),
-            pltpu.VMEM((nz - 1, 2, tiles, 8, 128), F32),
-            pltpu.VMEM((plane, 2 * share, 128), F32),
-            pltpu.VMEM((plane - 1, 2 * share, 128), F32),
-            pltpu.VMEM((plane, 2 * share, 128), F32),
-            pltpu.VMEM((2, tiles, 8, 128), F32),
+            pltpu.VMEM((group, 2, 8, 128), F32),
+            pltpu.VMEM((2, group - 1, 8, 128), F32),
+            pltpu.VMEM((2, 8, 128), F32),
+            pltpu.VMEM((2, planes, 8, 128), F32),
+            pltpu.VMEM((2, 8, 128), F32),
             dma((len(VOLUME),)), dma((len(VOLUME),)),
             dma((2,)), dma((2,)),
             dma((6,)), dma((6,)),
             dma((2, 2)), dma((2, 2)),
-            dma((2, nz - 1)), dma((2, nz - 1)),
-            dma((plane - 1,)), dma((plane - 1,)),
-            dma((plane - 1,)), dma((plane - 1,)),
-            dma((nz - 1,)), dma((nz - 1,)),
+            *[dma((2,))] * 6,
         ],
-        compiler_params=pltpu.CompilerParams(collective_id=0, has_side_effects=True),
+        compiler_params=pltpu.CompilerParams(collective_id=0, has_side_effects=True, vmem_limit_bytes=40 << 20),
         cost_estimate=pl.CostEstimate(flops=2000000000, bytes_accessed=2000000, transcendentals=400000),
-    )(volume, *flat)
+    )(*[far(array) for array in (volume, *flat)])
     jv, gv_first, gv_second = pl.pallas_call(
-        functools.partial(last_kernel, tiles, count_all, factor),
+        functools.partial(last_kernel, count_all, factor),
         out_shape=(
-            jax.ShapeDtypeStruct((chan, dx, dy, 128), BF16),
+            jax.ShapeDtypeStruct(volume.shape, BF16),
             jax.ShapeDtypeStruct((9, 3 * chan, chan), F32),
             jax.ShapeDtypeStruct((9, 3 * chan, chan), F32),
         ),
         in_specs=[vm] * 4,
         out_specs=(vm, vm, vm),
-    )(tot, jv_raw, flat[2], flat[3])
+        compiler_params=pltpu.CompilerParams(vmem_limit_bytes=8 << 20),
+    )(near(tot), near(jv_made), flat[2], flat[3])
     return (jv, gv_first.reshape(shape), gv_second.reshape(shape))
 
 

time: 68.7 us -> 58.2 us (0.85)
  Pallas kernels: 67.9 us -> 57.4 us
    pallas_call x2, Pallas kernels: 67.9 us -> 57.4 us  [the longest x1 56.2 us: body(): pl.pallas_call(functools.partial(main_kernel, nx, ny, nz, dx, dy), out_sh...]
where the time goes in v4:
time: 58.2 us; the launch traced here: 58.1 us
  Pallas kernels  57.4 us (99%)
  between operations  0.67 us (1%)
    pallas_call x1, Pallas kernels, body(): pl.pallas_call(functools.partial(main_kernel, nx, ny, nz, dx, dy), out_sh...  56.2 us
    pallas_call x1, Pallas kernels, body(): pl.pallas_call(functools.partial(last_kernel, count_all, factor), out_sha...  1.19 us

profile of v4, /device:TPU:1, one launch (start us, length us, event | category | flops | bytes accessed | tf_op | source)
XLA Modules:
  0.0 58.1 jit_solution(15400434889523754306)
XLA Ops:
  0.6 0.0 copy-start
  0.6 0.0 copy-start.1
  0.7 56.2 %shard_map.76 = (f32[32,2,8,128]{3,2,1,0:T(8,128)S(1)}, bf16[32,2,16,128]{3,2,1,0:T(8,128)(2,1)S(1)}) custom-call(bf16[32,2,16,128]{3,2,1,0:T(8,128)(2,1)} %vol_in.1, bf16[864,32]{1,0:T(8,128)(2,1)} %bitcast.12, bf16[864,32]{1,0:T(8,128)(2,1)} %bitcast.13, bf16[864,32]{1,0:T(8,128)(2,1)} %bitcast.6, bf16[864,32]{1,0:T(8,128)(2,1)} %bitcast.8), custom_call_target="tpu_custom_call" | custom-call | flops 2000000000 | bytes 2000000 | tf_op jit(solution)/shard_map/pallas_call | solution.py:559
  56.9 0.0 copy-done
  56.9 0.0 copy-done.1
  56.9 1.2 %shard_map.77 = (bf16[32,2,16,128]{3,2,1,0:T(8,128)(2,1)}, f32[9,96,32]{2,1,0:T(8,128)}, f32[9,96,32]{2,1,0:T(8,128)}) custom-call(f32[32,2,8,128]{3,2,1,0:T(8,128)S(1)} %get-tuple-element.8.tot, bf16[32,2,16,128]{3,2,1,0:T(8,128)(2,1)S(1)} %get-tuple-element.9.jv_in, bf16[864,32]{1,0:T(8,128)(2,1)S(1)} %bitcast.7, bf16[864,32]{1,0:T(8,128)(2,1)S(1)} %bitcast.9), custom_call_target="tpu_custom_call" | custom-call | tf_op jit(solution)/shard_map/pallas_call | solution.py:604
Async XLA Ops:
  0.6 56.2 %copy-start = (bf16[3,3,3,32,32]{4,3,2,1,0:T(8,128)(2,1)S(1)}, bf16[3,3,3,32,32]{4,3,2,1,0:T(8,128)(2,1)}, u32[]{:S(2)}) copy-start(bf16[3,3,3,32,32]{4,3,2,1,0:T(8,128)(2,1)} %param.8) | copy-start | bytes 165892
  0.6 56.2 %copy-start.1 = (bf16[3,3,3,32,32]{4,3,2,1,0:T(8,128)(2,1)S(1)}, bf16[3,3,3,32,32]{4,3,2,1,0:T(8,128)(2,1)}, u32[]{:S(2)}) copy-start(bf16[3,3,3,32,32]{4,3,2,1,0:T(8,128)(2,1)} %param.9) | copy-start | bytes 165892

commit v5 on v4

--- a/solution.py
+++ b/solution.py
@@ -63,14 +63,16 @@
     planes = high * nx
     col, row = lax.rem(iy, wide), iy // wide
     level = row * nx + ix
-    zs = [lax.rem(iz + d, nz) for d in range(nz)]
+    rings = nz // 2
+    core, ring = lax.rem(iz, 2), iz // 2
+    gs = [lax.rem(ring + d, rings) for d in range(rings)]
     cs = [lax.rem(col + d, wide) for d in range(wide)]
-    turns = [(ez, ec) for ez in range(nz) for ec in range(wide)][1:]
-    me = iz * wide + col
-
-    def a_peer(n):
-        ez, ec = turns[n]
-        return {"gx": ix, "gy": row * wide + cs[ec], "gz": zs[ez]}
+    turns = [(eg, ec) for eg in range(rings) for ec in range(wide)]
+    me = ring * wide + col
+
+    def a_peer(n, side):
+        eg, ec = turns[n]
+        return {"gx": ix, "gy": row * wide + cs[ec], "gz": 2 * gs[eg] + side}
 
     def z_peer(d):
         other = lax.rem(level + d, planes)
@@ -99,8 +101,10 @@
 
     for d in range(1, planes):
         greet(z_peer(d))
-    for n in range(len(turns)):
-        greet(a_peer(n))
+    for n in range(1, len(turns)):
+        greet(a_peer(n, 0))
+        greet(a_peer(n, 1))
+    greet(a_peer(0, 1 - core))
     for o in OFFSETS:
         guarded(there(*o), lambda: greet(at(*o)))
 
@@ -117,10 +121,16 @@
         return first, last
 
     blank = jnp.zeros((chan, 128), BF16)
-    edges = (blank, blank)
+    half_lane = lane[0:16]
+    edges = [blank[0:16], blank[0:16]]
     for x in range(dx):
         for y in range(dy):
-            edges = packed(r1[dx + x, 3 + y], x * dy + y, edges)
+            raw = r1[dx + x, 3 + y]
+            for part_of in range(2):
+                piece = raw[16 * part_of : 16 * part_of + 16]
+                here = half_lane == x * dy + y + 64 * part_of
+                for n, column in enumerate((piece[:, 0:1], piece[:, 127:128])):
+                    edges[n] = jnp.where(here, jnp.broadcast_to(column, piece.shape), edges[n])
     pk1[0], pk1[1] = edges
 
     @pl.when(ix == 0)
@@ -163,7 +173,7 @@
         return 3 - (index == 0).astype(jnp.int32) - (index == count - 1).astype(jnp.int32)
 
     near = span(ix, nx) * span(iy, ny) * span(iz, nz) - 1
-    pl.semaphore_wait(barrier, near + planes - 1 + len(turns))
+    pl.semaphore_wait(barrier, near + planes - 1 + 2 * len(turns) - 1)
 
     def send_vol(n):
         (ox, oy, oz), far = VOLUME[n]
@@ -215,8 +225,8 @@
 
     def shift(raw_ref, out_ref, x, y, left, right, j):
         raw = raw_ref[x, y]
-        before = left if j == 0 else pltpu.roll(left, 128 - j, 1)
-        after = right if j == 127 else pltpu.roll(right, 127 - j, 1)
+        before = left if not j else pltpu.roll(left, 128 - j, 1)
+        after = right if j is None else pltpu.roll(right, 127 - j, 1)
         out_ref[x, y, 0:chan] = jnp.where(lane == 0, before, pltpu.roll(raw, 1, 1))
         out_ref[x, y, chan:two] = jnp.where(lane == 127, after, pltpu.roll(raw, 127, 1))
 
@@ -226,16 +236,21 @@
         out_ref[x, y, chan:two] = pltpu.roll(raw, 127, 1)
 
     def patch(out_ref, x, y, left, right, j):
-        before = left if j == 0 else pltpu.roll(left, 128 - j, 1)
-        after = right if j == 127 else pltpu.roll(right, 127 - j, 1)
+        before = left if not j else pltpu.roll(left, 128 - j, 1)
+        after = right if j is None else pltpu.roll(right, 127 - j, 1)
         out_ref[x, y, 0:chan] = jnp.where(lane == 0, before, out_ref[x, y, 0:chan])
         out_ref[x, y, chan:two] = jnp.where(lane == 127, after, out_ref[x, y, chan:two])
+
+    def spread(tile, j, to):
+        shifts = [(to - j - 64 * part_of) % 128 for part_of in range(2)]
+        return jnp.concatenate([pltpu.roll(tile, k, 1) if k else tile for k in shifts], axis=0)
 
     def slab1(which, lines, turned=False):
         for x in which:
             for y in lines:
                 bx, by = x // dx, (y + dy - 3) // dy
-                place = (ed1[0, bx, by], ed1[1, bx, by], (x % dx) * dy + (y + dy - 3) % dy)
+                j = (x % dx) * dy + (y + dy - 3) % dy
+                place = (spread(ed1[0, bx, by], j, 0), spread(ed1[1, bx, by], j, 127), None)
                 if turned:
                     patch(q1, x, y, *place)
                 else:
@@ -390,51 +405,89 @@
     lane8 = lax.broadcasted_iota(jnp.int32, (8, 128), 1)
 
     def put_part(f, value):
-        for t in range(nz * wide):
+        for t in range(2 * len(turns)):
             if t < 27:
                 j, s = t // 9, t % 9
                 tail = pltpu.roll(value[216 + 8 * s : 224 + 8 * s], 96 - 32 * j, 1)
-                part[t, f] = jnp.where(lane8 < 96, value[8 * t : 8 * t + 8], tail)
+                part[t // 2, f, t % 2] = jnp.where(lane8 < 96, value[8 * t : 8 * t + 8], tail)
             else:
-                part[t, f] = jnp.zeros((8, 128), F32)
+                part[t // 2, f, t % 2] = jnp.zeros((8, 128), F32)
 
     def send_a(f, n):
-        ez, ec = turns[n]
-        return copy(part.at[zs[ez] * wide + cs[ec], f], recv_a.at[f, n], sa.at[f], ra.at[f], a_peer(n))
+        eg, ec = turns[n]
+        return copy(
+            part.at[gs[eg] * wide + cs[ec], f], recv_a.at[f, core * len(turns) + n], sa.at[f], ra.at[f], a_peer(n, 1)
+        )
 
     def send_z(f, d):
         return copy(sum_a.at[f], recv_z.at[f, level], sz.at[f], rz.at[f], z_peer(d))
 
-    def send_g(f, n):
-        return copy(fin.at[f], tot.at[me, f], sg.at[f], rg.at[f], a_peer(n))
+    def send_g(f, n, side):
+        return copy(fin.at[f], tot.at[me, f], sg.at[f], rg.at[f], a_peer(n, side))
 
     def settle(ref, sem):
         pltpu.make_async_copy(ref, ref, sem).wait()
 
+    count = len(turns)
+
     def start_a(f, value):
         put_part(f, value)
-        for n in range(len(turns)):
+        for n in range(1, count):
             send_a(f, n).start()
 
+        @pl.when(core == 0)
+        def _():
+            send_a(f, 0).start()
+
+        @pl.when(core == 1)
+        def _():
+            recv_a[f, count] = part[me, f]
+
     def start_z(f):
-        settle(recv_a.at[f], ra.at[f])
-        total = part[me, f]
-        for n in range(len(turns)):
-            total = total + recv_a[f, n]
-        sum_a[f] = total
-        for d in range(1, planes):
-            send_z(f, d).start()
-        recv_z[f, level] = total
+        @pl.when(core == 1)
+        def _():
+            settle(recv_a.at[f, 1 : 2 * count], ra.at[f])
+            total = recv_a[f, 0]
+            for n in range(1, 2 * count):
+                total = total + recv_a[f, n]
+            sum_a[f] = total
+            for d in range(1, planes):
+                send_z(f, d).start()
+            recv_z[f, level] = total
 
     def start_g(f):
-        settle(recv_z.at[f, 1:planes], rz.at[f])
-        total = recv_z[f, 0]
-        for d in range(1, planes):
-            total = total + recv_z[f, d]
-        fin[f] = total
-        for n in range(len(turns)):
-            send_g(f, n).start()
-        tot[me, f] = total
+        @pl.when(core == 1)
+        def _():
+            settle(recv_z.at[f, 1:planes], rz.at[f])
+            total = recv_z[f, 0]
+            for d in range(1, planes):
+                total = total + recv_z[f, d]
+            fin[f] = total
+            for n in range(1, count):
+                send_g(f, n, 0).start()
+                send_g(f, n, 1).start()
+            send_g(f, 0, 0).start()
+            tot[me, f] = total
+
+    def end_g(f):
+        @pl.when(core == 1)
+        def _():
+            settle(recv_a.at[f, 1:count], rg.at[f])
+
+        @pl.when(core == 0)
+        def _():
+            settle(recv_a.at[f, 0:count], rg.at[f])
+
+    def leave(f):
+        @pl.when(core == 1)
+        def _():
+            settle(recv_a.at[f, 1:count], sa.at[f])
+            settle(recv_z.at[f, 1:planes], sz.at[f])
+            settle(recv_a.at[f, 1 : 2 * count], sg.at[f])
+
+        @pl.when(core == 0)
+        def _():
+            settle(recv_a.at[f, 0:count], sa.at[f])
 
     start_a(0, correlate(r2.at[1], q2.at[1], 0, 1, ej))
 
@@ -499,15 +552,15 @@
 
     lax.fori_loop(0, dy // 2, halo3, 0, unroll=4)
 
+    start_a(1, correlate(r1, q1, 1, 2, eb))
     start_z(0)
-    start_a(1, correlate(r1, q1, 1, 2, eb))
     for x in range(dx):
         jv_out[:, x] = jnp.transpose(r3[x + 1, 1 : 1 + dy], (1, 0, 2))
     start_g(0)
     start_z(1)
     start_g(1)
     for f in range(2):
-        settle(recv_a.at[f], rg.at[f])
+        end_g(f)
 
     for n, (o, _) in enumerate(VOLUME):
         guarded(there(*o), lambda: send_vol(n).wait_send())
@@ -519,15 +572,13 @@
     for n, (ox, oz) in enumerate(SIDES):
         guarded(there(ox, 0, oz), lambda: send_jv(n).wait_send())
     for f in range(2):
-        settle(recv_a.at[f], sa.at[f])
-        settle(recv_a.at[f], sg.at[f])
-        settle(recv_z.at[f, 1:planes], sz.at[f])
+        leave(f)
 
 
 def last_kernel(count_all, factor, tot, jv_in, v_first, v_second, jv, gv_first, gv_second):
     jv[...] = jv_in[...]
     for f, (v_ref, out) in enumerate(((v_second, gv_second), (v_first, gv_first))):
-        tile = [tot[t, f] for t in range(27)]
+        tile = [tot[t // 2, f, t % 2] for t in range(27)]
         for kx in range(3):
             for ky in range(3):
                 pieces = []
@@ -546,7 +597,7 @@
 def body(volume, w_first, w_second, v_first, v_second):
     chan, dx, dy, dz = volume.shape
     nx, ny, nz = lax.axis_size("gx"), lax.axis_size("gy"), lax.axis_size("gz")
-    group = 4 * nz
+    group = 2 * nz
     planes = nx * ny // 4
     count_all = float(dx * dy * dz * nx * ny * nz)
     factor = math.sqrt(27.0 * chan)
@@ -559,7 +610,7 @@
     tot, jv_made = pl.pallas_call(
         functools.partial(main_kernel, nx, ny, nz, dx, dy),
         out_shape=(
-            pltpu.VMEM((group, 2, 8, 128), F32),
+            pltpu.VMEM((group, 2, 2, 8, 128), F32),
             pltpu.VMEM((chan, dx, dy, 128), BF16),
         ),
         in_specs=[pl.BlockSpec(memory_space=pltpu.HBM)] * 5,
@@ -581,17 +632,17 @@
             pltpu.VMEM((2 * chan, 27 * chan), BF16),
             pltpu.VMEM((3 * chan, 18 * chan), BF16),
             pltpu.VMEM((3 * chan, 9 * chan), BF16),
-            pltpu.VMEM((2, chan, 128), BF16),
-            pltpu.VMEM((2, 3, 3, chan, 128), BF16),
+            pltpu.VMEM((2, 16, 128), BF16),
+            pltpu.VMEM((2, 3, 3, 16, 128), BF16),
             pltpu.VMEM((2, 2, chan, 128), BF16),
             pltpu.VMEM((2, 2, chan, 128), BF16),
             pltpu.VMEM((2, chan, 128), BF16),
             pltpu.VMEM((2, 3, chan, 128), BF16),
-            pltpu.VMEM((group, 2, 8, 128), F32),
-            pltpu.VMEM((2, group - 1, 8, 128), F32),
-            pltpu.VMEM((2, 8, 128), F32),
-            pltpu.VMEM((2, planes, 8, 128), F32),
-            pltpu.VMEM((2, 8, 128), F32),
+            pltpu.VMEM((group, 2, 2, 8, 128), F32),
+            pltpu.VMEM((2, 2 * group, 2, 8, 128), F32),
+            pltpu.VMEM((2, 2, 8, 128), F32),
+            pltpu.VMEM((2, planes, 2, 8, 128), F32),
+            pltpu.VMEM((2, 2, 8, 128), F32),
             dma((len(VOLUME),)), dma((len(VOLUME),)),
             dma((2,)), dma((2,)),
             dma((6,)), dma((6,)),

time: 58.2 us -> 55.6 us (0.955)
  Pallas kernels: 57.4 us -> 54.8 us
    pallas_call x1, Pallas kernels: 56.2 us -> 53.6 us  [body(): pl.pallas_call(functools.partial(main_kernel, nx, ny, nz, dx, dy), out_sh...]
where the time goes in v5:
time: 55.6 us; the launch traced here: 55.5 us
  Pallas kernels  54.8 us (99%)
  between operations  0.67 us (1%)
    pallas_call x1, Pallas kernels, body(): pl.pallas_call(functools.partial(main_kernel, nx, ny, nz, dx, dy), out_sh...  53.6 us
    pallas_call x1, Pallas kernels, body(): pl.pallas_call(functools.partial(last_kernel, count_all, factor), out_sha...  1.19 us

profile of v5, /device:TPU:1, one launch (start us, length us, event | category | flops | bytes accessed | tf_op | source)
XLA Modules:
  0.0 55.5 jit_solution(3167814322851924905)
XLA Ops:
  0.6 0.0 copy-start
  0.6 0.0 copy-start.1
  0.7 53.6 %shard_map.76 = (f32[16,2,2,8,128]{4,3,2,1,0:T(8,128)S(1)}, bf16[32,2,16,128]{3,2,1,0:T(8,128)(2,1)S(1)}) custom-call(bf16[32,2,16,128]{3,2,1,0:T(8,128)(2,1)} %vol_in.1, bf16[864,32]{1,0:T(8,128)(2,1)} %bitcast.12, bf16[864,32]{1,0:T(8,128)(2,1)} %bitcast.13, bf16[864,32]{1,0:T(8,128)(2,1)} %bitcast.6, bf16[864,32]{1,0:T(8,128)(2,1)} %bitcast.8), custom_call_target="tpu_custom_call" | custom-call | flops 2000000000 | bytes 2000000 | tf_op jit(solution)/shard_map/pallas_call | solution.py:610
  54.3 0.0 copy-done
  54.3 0.0 copy-done.1
  54.3 1.2 %shard_map.77 = (bf16[32,2,16,128]{3,2,1,0:T(8,128)(2,1)}, f32[9,96,32]{2,1,0:T(8,128)}, f32[9,96,32]{2,1,0:T(8,128)}) custom-call(f32[16,2,2,8,128]{4,3,2,1,0:T(8,128)S(1)} %get-tuple-element.8.tot, bf16[32,2,16,128]{3,2,1,0:T(8,128)(2,1)S(1)} %get-tuple-element.9.jv_in, bf16[864,32]{1,0:T(8,128)(2,1)S(1)} %bitcast.7, bf16[864,32]{1,0:T(8,128)(2,1)S(1)} %bitcast.9), custom_call_target="tpu_custom_call" | custom-call | tf_op jit(solution)/shard_map/pallas_call | solution.py:655
Async XLA Ops:
  0.6 53.7 %copy-start = (bf16[3,3,3,32,32]{4,3,2,1,0:T(8,128)(2,1)S(1)}, bf16[3,3,3,32,32]{4,3,2,1,0:T(8,128)(2,1)}, u32[]{:S(2)}) copy-start(bf16[3,3,3,32,32]{4,3,2,1,0:T(8,128)(2,1)} %param.8) | copy-start | bytes 165892
  0.6 53.7 %copy-start.1 = (bf16[3,3,3,32,32]{4,3,2,1,0:T(8,128)(2,1)S(1)}, bf16[3,3,3,32,32]{4,3,2,1,0:T(8,128)(2,1)}, u32[]{:S(2)}) copy-start(bf16[3,3,3,32,32]{4,3,2,1,0:T(8,128)(2,1)} %param.9) | copy-start | bytes 165892

commit v6 on v5

--- a/solution.py
+++ b/solution.py
@@ -13,8 +13,10 @@
 BF16 = jnp.bfloat16
 F32 = jnp.float32
 OFFSETS = [o for o in itertools.product((-1, 0, 1), repeat=3) if o != (0, 0, 0)]
-VOLUME = [(o, False) for o in OFFSETS if o[1] != 0 and o[2] == 0]
+VOLUME = []
 VOLUME += [(o, False) for o in OFFSETS if o[1] != 0 and o[2] != 0]
+VOLUME += [(o, False) for o in OFFSETS if o[1] != 0 and o[0] == 0 and o[2] == 0]
+VOLUME += [(o, False) for o in OFFSETS if o[1] != 0 and o[0] != 0 and o[2] == 0]
 VOLUME += [((ox, 0, 0), False) for ox in (-1, 1)]
 VOLUME += [((ox, 0, oz), False) for ox in (0, -1, 1) for oz in (-1, 1)]
 VOLUME += [((ox, 0, 0), True) for ox in (-1, 1)]
@@ -67,7 +69,11 @@
     core, ring = lax.rem(iz, 2), iz // 2
     gs = [lax.rem(ring + d, rings) for d in range(rings)]
     cs = [lax.rem(col + d, wide) for d in range(wide)]
-    turns = [(eg, ec) for eg in range(rings) for ec in range(wide)]
+    turns = sorted(
+        ((eg, ec) for eg in range(rings) for ec in range(wide)),
+        key=lambda t: (t != (0, 0), -min(t[0], rings - t[0]) - min(t[1], wide - t[1])),
+    )
+    steps = sorted(range(1, planes), key=lambda d: -min(d, planes - d))
     me = ring * wide + col
 
     def a_peer(n, side):
@@ -99,10 +105,14 @@
     def greet(peer):
         pl.semaphore_signal(barrier, inc=1, device_id=peer, device_id_type=MESH)
 
-    for d in range(1, planes):
-        greet(z_peer(d))
+    @pl.when(core == 1)
+    def _():
+        for d in range(1, planes):
+            greet(z_peer(d))
+        for n in range(1, len(turns)):
+            greet(a_peer(n, 0))
+
     for n in range(1, len(turns)):
-        greet(a_peer(n, 0))
         greet(a_peer(n, 1))
     greet(a_peer(0, 1 - core))
     for o in OFFSETS:
@@ -173,7 +183,7 @@
         return 3 - (index == 0).astype(jnp.int32) - (index == count - 1).astype(jnp.int32)
 
     near = span(ix, nx) * span(iy, ny) * span(iz, nz) - 1
-    pl.semaphore_wait(barrier, near + planes - 1 + 2 * len(turns) - 1)
+    pl.semaphore_wait(barrier, near + len(turns) + core * (planes - 1 + len(turns) - 1))
 
     def send_vol(n):
         (ox, oy, oz), far = VOLUME[n]
@@ -297,7 +307,7 @@
     take_vol(lambda o, far: o[0] != 0 and o[1] == 0 and not far)
     slab1((dx - 1, 2 * dx), own_y)
     edges = lax.fori_loop(
-        0, dx * inner, lambda i, c: layer1(1 + i // inner, 4 + 2 * lax.rem(i, inner), c), (blank,) * 4, unroll=6
+        0, dx * inner, lambda i, c: layer1(1 + i // inner, 4 + 2 * lax.rem(i, inner), c), (blank,) * 4, unroll=dx * inner
     )
     take_vol(lambda o, far: o[1] != 0)
     slab1(range(1, 3 * dx - 1), halo_y)
@@ -311,7 +321,7 @@
     slab1((0, 3 * dx - 1), range(dy + 6))
     pairs = hy // 2
     edges = lax.fori_loop(
-        0, 2 * pairs, lambda i, c: layer1((hx - 1) * (i // pairs), 2 * lax.rem(i, pairs), c), edges, unroll=10
+        0, 2 * pairs, lambda i, c: layer1((hx - 1) * (i // pairs), 2 * lax.rem(i, pairs), c), edges, unroll=2 * pairs
     )
     pk2[0, 0], pk2[1, 0], pk2[0, 1], pk2[1, 1] = edges
 
@@ -358,28 +368,31 @@
                 carry = packed(value, x * (dy + 2) + y + half, carry)
         return carry
 
-    cut = 2 * ((dy + 2 + 2) // 4)
+    cuts = [0, 8, 14, dy + 2]
 
     def send_plane(n, ox, late):
-        lines = slice(cut, dy + 2) if late else slice(0, cut)
+        lines = slice(cuts[late], cuts[late + 1])
         return copy(
             r3.at[1 if ox < 0 else dx, lines], r3.at[dx + 1 if ox < 0 else 0, lines],
-            ps3.at[n, int(late)], pr3.at[n, int(late)], at(ox, 0, 0),
+            ps3.at[n, late], pr3.at[n, late], at(ox, 0, 0),
         )
 
     def send_jv(n):
         ox, oz = SIDES[n]
         return copy(pk3.at[1 if oz > 0 else 0], ed3.at[0 if oz > 0 else 1, 1 - ox], xs3.at[n], xr3.at[n], at(ox, 0, oz))
 
-    edges = lax.fori_loop(0, cut // 2, layer2, (blank, blank), unroll=cut // 2)
-    for n, ox in enumerate((-1, 1)):
-        guarded(there(ox, 0, 0), lambda: send_plane(n, ox, False).start())
-    rest = (dy + 2 - cut) // 2
-    pk3[0], pk3[1] = lax.fori_loop(0, rest, lambda i, c: layer2(cut // 2 + i, c), edges, unroll=rest)
+    edges = (blank, blank)
+    for late in range(3):
+        first, count2 = cuts[late] // 2, (cuts[late + 1] - cuts[late]) // 2
+        edges = lax.fori_loop(0, count2, lambda i, c: layer2(first + i, c), edges, unroll=count2)
+        if late < 2:
+            for n, ox in enumerate((-1, 1)):
+                guarded(there(ox, 0, 0), lambda: send_plane(n, ox, late).start())
+    pk3[0], pk3[1] = edges
     for n, (ox, oz) in enumerate(SIDES):
         guarded(there(ox, 0, oz), lambda: send_jv(n).start())
     for n, ox in enumerate((-1, 1)):
-        guarded(there(ox, 0, 0), lambda: send_plane(n, ox, True).start())
+        guarded(there(ox, 0, 0), lambda: send_plane(n, ox, 2).start())
 
     for x in range(dx):
         own = r3[x + 1, 1 : 1 + dy]
@@ -451,7 +464,7 @@
             for n in range(1, 2 * count):
                 total = total + recv_a[f, n]
             sum_a[f] = total
-            for d in range(1, planes):
+            for d in steps:
                 send_z(f, d).start()
             recv_z[f, level] = total
 
@@ -536,7 +549,7 @@
     lax.fori_loop(0, dy // 2, own3, 0, unroll=4)
     take_jv(False)
     for n, ox in enumerate((-1, 1)):
-        for late in (False, True):
+        for late in range(3):
             guarded(there(-ox, 0, 0), lambda: send_plane(n, ox, late).wait_recv())
     slab3((0, dx + 1))
 
@@ -567,7 +580,7 @@
     for n, oz in enumerate((-1, 1)):
         guarded(there(0, 0, oz), lambda: send_hid(n, oz).wait_send())
     for n, ox in enumerate((-1, 1)):
-        for late in (False, True):
+        for late in range(3):
             guarded(there(ox, 0, 0), lambda: send_plane(n, ox, late).wait_send())
     for n, (ox, oz) in enumerate(SIDES):
         guarded(there(ox, 0, oz), lambda: send_jv(n).wait_send())
@@ -646,7 +659,7 @@
             dma((len(VOLUME),)), dma((len(VOLUME),)),
             dma((2,)), dma((2,)),
             dma((6,)), dma((6,)),
-            dma((2, 2)), dma((2, 2)),
+            dma((2, 3)), dma((2, 3)),
             *[dma((2,))] * 6,
         ],
         compiler_params=pltpu.CompilerParams(collective_id=0, has_side_effects=True, vmem_limit_bytes=40 << 20),

time: 55.6 us -> 52.5 us (0.944)
  Pallas kernels: 54.8 us -> 51.7 us
    pallas_call x1, Pallas kernels: 53.6 us -> 50.6 us  [body(): pl.pallas_call(functools.partial(main_kernel, nx, ny, nz, dx, dy), out_sh...]
where the time goes in v6:
time: 52.5 us; the launch traced here: 52.4 us
  Pallas kernels  51.7 us (98%)
  between operations  0.67 us (1%)
    pallas_call x1, Pallas kernels, body(): pl.pallas_call(functools.partial(main_kernel, nx, ny, nz, dx, dy), out_sh...  50.6 us
    pallas_call x1, Pallas kernels, body(): pl.pallas_call(functools.partial(last_kernel, count_all, factor), out_sha...  1.19 us

profile of v6, /device:TPU:1, one launch (start us, length us, event | category | flops | bytes accessed | tf_op | source)
XLA Modules:
  0.0 52.4 jit_solution(16607697545251555362)
XLA Ops:
  0.6 0.0 copy-start
  0.6 0.0 copy-start.1
  0.7 50.6 %shard_map.76 = (f32[16,2,2,8,128]{4,3,2,1,0:T(8,128)S(1)}, bf16[32,2,16,128]{3,2,1,0:T(8,128)(2,1)S(1)}) custom-call(bf16[32,2,16,128]{3,2,1,0:T(8,128)(2,1)} %vol_in.1, bf16[864,32]{1,0:T(8,128)(2,1)} %bitcast.12, bf16[864,32]{1,0:T(8,128)(2,1)} %bitcast.13, bf16[864,32]{1,0:T(8,128)(2,1)} %bitcast.6, bf16[864,32]{1,0:T(8,128)(2,1)} %bitcast.8), custom_call_target="tpu_custom_call" | custom-call | flops 2000000000 | bytes 2000000 | tf_op jit(solution)/shard_map/pallas_call | solution.py:623
  51.2 0.0 copy-done
  51.2 0.0 copy-done.1
  51.2 1.2 %shard_map.77 = (bf16[32,2,16,128]{3,2,1,0:T(8,128)(2,1)}, f32[9,96,32]{2,1,0:T(8,128)}, f32[9,96,32]{2,1,0:T(8,128)}) custom-call(f32[16,2,2,8,128]{4,3,2,1,0:T(8,128)S(1)} %get-tuple-element.8.tot, bf16[32,2,16,128]{3,2,1,0:T(8,128)(2,1)S(1)} %get-tuple-element.9.jv_in, bf16[864,32]{1,0:T(8,128)(2,1)S(1)} %bitcast.7, bf16[864,32]{1,0:T(8,128)(2,1)S(1)} %bitcast.9), custom_call_target="tpu_custom_call" | custom-call | tf_op jit(solution)/shard_map/pallas_call | solution.py:668
Async XLA Ops:
  0.6 50.6 %copy-start = (bf16[3,3,3,32,32]{4,3,2,1,0:T(8,128)(2,1)S(1)}, bf16[3,3,3,32,32]{4,3,2,1,0:T(8,128)(2,1)}, u32[]{:S(2)}) copy-start(bf16[3,3,3,32,32]{4,3,2,1,0:T(8,128)(2,1)} %param.8) | copy-start | bytes 165892
  0.6 50.6 %copy-start.1 = (bf16[3,3,3,32,32]{4,3,2,1,0:T(8,128)(2,1)S(1)}, bf16[3,3,3,32,32]{4,3,2,1,0:T(8,128)(2,1)}, u32[]{:S(2)}) copy-start(bf16[3,3,3,32,32]{4,3,2,1,0:T(8,128)(2,1)} %param.9) | copy-start | bytes 165892

commit v7 on v6

--- a/solution.py
+++ b/solution.py
@@ -17,8 +17,8 @@
 VOLUME += [(o, False) for o in OFFSETS if o[1] != 0 and o[2] != 0]
 VOLUME += [(o, False) for o in OFFSETS if o[1] != 0 and o[0] == 0 and o[2] == 0]
 VOLUME += [(o, False) for o in OFFSETS if o[1] != 0 and o[0] != 0 and o[2] == 0]
+VOLUME += [((ox, 0, oz), False) for ox in (0, -1, 1) for oz in (-1, 1)]
 VOLUME += [((ox, 0, 0), False) for ox in (-1, 1)]
-VOLUME += [((ox, 0, oz), False) for ox in (0, -1, 1) for oz in (-1, 1)]
 VOLUME += [((ox, 0, 0), True) for ox in (-1, 1)]
 SIDES = [(ox, oz) for ox in (-1, 0, 1) for oz in (-1, 1)]
 
@@ -131,28 +131,30 @@
         return first, last
 
     blank = jnp.zeros((chan, 128), BF16)
-    half_lane = lane[0:16]
-    edges = [blank[0:16], blank[0:16]]
+    half_lane = lane[0:8]
+    edges = [blank[0:8], blank[0:8]]
     for x in range(dx):
         for y in range(dy):
             raw = r1[dx + x, 3 + y]
-            for part_of in range(2):
-                piece = raw[16 * part_of : 16 * part_of + 16]
-                here = half_lane == x * dy + y + 64 * part_of
+            for part_of in range(4):
+                piece = raw[8 * part_of : 8 * part_of + 8]
+                here = half_lane == x * dy + y + 32 * part_of
                 for n, column in enumerate((piece[:, 0:1], piece[:, 127:128])):
                     edges[n] = jnp.where(here, jnp.broadcast_to(column, piece.shape), edges[n])
     pk1[0], pk1[1] = edges
 
     @pl.when(ix == 0)
     def _():
-        zero(r1.at[0:dx])
+        zero(r1.at[dx - 1])
+        zero(r2.at[:, 0])
         zero(ed1.at[:, 0])
         zero(r3.at[0])
         zero(ed3.at[:, 0])
 
     @pl.when(ix == nx - 1)
     def _():
-        zero(r1.at[2 * dx : 3 * dx])
+        zero(r1.at[2 * dx])
+        zero(r2.at[:, hx - 1])
         zero(ed1.at[:, 2])
         zero(r3.at[dx + 1])
         zero(ed3.at[:, 2])
@@ -201,7 +203,7 @@
             to = dx * (1 - ox)
             src = r1.at[dx : 2 * dx, src_y : src_y + 3]
             dst = r1.at[to : to + dx, dst_y : dst_y + 3]
-        return copy(src, dst, xs1.at[n], xr1.at[n], at(ox, oy, oz))
+        return copy(src, dst, xs1.at[0], xr1.at[n], at(ox, oy, oz))
 
     def back(o):
         return there(*(-c for c in o))
@@ -252,7 +254,7 @@
         out_ref[x, y, chan:two] = jnp.where(lane == 127, after, out_ref[x, y, chan:two])
 
     def spread(tile, j, to):
-        shifts = [(to - j - 64 * part_of) % 128 for part_of in range(2)]
+        shifts = [(to - j - 32 * part_of) % 128 for part_of in range(4)]
         return jnp.concatenate([pltpu.roll(tile, k, 1) if k else tile for k in shifts], axis=0)
 
     def slab1(which, lines, turned=False):
@@ -298,31 +300,47 @@
 
     own_y = range(3, 3 + dy)
     halo_y = [*range(3), *range(3 + dy, 6 + dy)]
-    inner = (dy - 4) // 2
+    pairs = hy // 2
+
+    def line1(x, carry):
+        return lax.fori_loop(0, pairs, lambda i, c: layer1(x, 2 * i, c), carry, unroll=pairs)
+
+    def low_near():
+        take_vol(lambda o, far: o == (1, 0, 0) and not far)
+        slab1((dx - 1,), own_y)
+
+    def high_near():
+        take_vol(lambda o, far: o == (-1, 0, 0) and not far)
+        slab1((2 * dx,), own_y)
+
+    low_first = ix == 0
+    first = jnp.where(low_first, 1, 2)
     for x in range(dx, 2 * dx):
         for y in own_y:
             turn(r1, q1, x, y)
-    take_vol(lambda o, far: o[0] == 0 and o[1] == 0)
+    take_vol(lambda o, far: o[1] == 0 and o[2] != 0)
     slab1(range(dx, 2 * dx), own_y, True)
-    take_vol(lambda o, far: o[0] != 0 and o[1] == 0 and not far)
-    slab1((dx - 1, 2 * dx), own_y)
-    edges = lax.fori_loop(
-        0, dx * inner, lambda i, c: layer1(1 + i // inner, 4 + 2 * lax.rem(i, inner), c), (blank,) * 4, unroll=dx * inner
-    )
+    guarded(low_first, low_near)
+    guarded(jnp.logical_not(low_first), high_near)
     take_vol(lambda o, far: o[1] != 0)
     slab1(range(1, 3 * dx - 1), halo_y)
-
-    def outer(i, c):
-        k = lax.rem(i, 4)
-        return layer1(1 + i // 4, 2 * lax.rem(k, 2) + dy * (k // 2), c)
-
-    edges = lax.fori_loop(0, dx * 4, outer, edges, unroll=8)
-    take_vol(lambda o, far: far)
-    slab1((0, 3 * dx - 1), range(dy + 6))
-    pairs = hy // 2
-    edges = lax.fori_loop(
-        0, 2 * pairs, lambda i, c: layer1((hx - 1) * (i // pairs), 2 * lax.rem(i, pairs), c), edges, unroll=2 * pairs
-    )
+    edges = line1(first, (blank,) * 4)
+    guarded(low_first, high_near)
+    guarded(jnp.logical_not(low_first), low_near)
+    edges = line1(3 - first, edges)
+
+    def low_end(carry):
+        take_vol(lambda o, far: far and o[0] > 0)
+        slab1((0,), range(dy + 6))
+        return line1(0, carry)
+
+    def high_end(carry):
+        take_vol(lambda o, far: far and o[0] < 0)
+        slab1((3 * dx - 1,), range(dy + 6))
+        return line1(hx - 1, carry)
+
+    edges = lax.cond(there(-1, 0, 0), low_end, lambda c: c, edges)
+    edges = lax.cond(there(1, 0, 0), high_end, lambda c: c, edges)
     pk2[0, 0], pk2[1, 0], pk2[0, 1], pk2[1, 1] = edges
 
     def send_hid(n, oz):
@@ -645,8 +663,8 @@
             pltpu.VMEM((2 * chan, 27 * chan), BF16),
             pltpu.VMEM((3 * chan, 18 * chan), BF16),
             pltpu.VMEM((3 * chan, 9 * chan), BF16),
-            pltpu.VMEM((2, 16, 128), BF16),
-            pltpu.VMEM((2, 3, 3, 16, 128), BF16),
+            pltpu.VMEM((2, 8, 128), BF16),
+            pltpu.VMEM((2, 3, 3, 8, 128), BF16),
             pltpu.VMEM((2, 2, chan, 128), BF16),
             pltpu.VMEM((2, 2, chan, 128), BF16),
             pltpu.VMEM((2, chan, 128), BF16),
@@ -656,7 +674,7 @@
             pltpu.VMEM((2, 2, 8, 128), F32),
             pltpu.VMEM((2, planes, 2, 8, 128), F32),
             pltpu.VMEM((2, 2, 8, 128), F32),
-            dma((len(VOLUME),)), dma((len(VOLUME),)),
+            dma((1,)), dma((len(VOLUME),)),
             dma((2,)), dma((2,)),
             dma((6,)), dma((6,)),
             dma((2, 3)), dma((2, 3)),

time: 52.5 us -> 52 us (level)
    pallas_call x1, Pallas kernels: 50.6 us -> 50 us  [body(): pl.pallas_call(functools.partial(main_kernel, nx, ny, nz, dx, dy), out_sh...]
where the time goes in v7:
time: 52 us; the launch traced here: 51.9 us
  Pallas kernels  51.2 us (98%)
  between operations  0.67 us (1%)
    pallas_call x1, Pallas kernels, body(): pl.pallas_call(functools.partial(main_kernel, nx, ny, nz, dx, dy), out_sh...  50 us
    pallas_call x1, Pallas kernels, body(): pl.pallas_call(functools.partial(last_kernel, count_all, factor), out_sha...  1.19 us

profile of v7, /device:TPU:1, one launch (start us, length us, event | category | flops | bytes accessed | tf_op | source)
XLA Modules:
  0.0 51.9 jit_solution(2259760308965611997)
XLA Ops:
  0.6 0.0 copy-start
  0.6 0.0 copy-start.1
  0.7 50.0 %shard_map.76 = (f32[16,2,2,8,128]{4,3,2,1,0:T(8,128)S(1)}, bf16[32,2,16,128]{3,2,1,0:T(8,128)(2,1)S(1)}) custom-call(bf16[32,2,16,128]{3,2,1,0:T(8,128)(2,1)} %vol_in.1, bf16[864,32]{1,0:T(8,128)(2,1)} %bitcast.12, bf16[864,32]{1,0:T(8,128)(2,1)} %bitcast.13, bf16[864,32]{1,0:T(8,128)(2,1)} %bitcast.6, bf16[864,32]{1,0:T(8,128)(2,1)} %bitcast.8), custom_call_target="tpu_custom_call" | custom-call | flops 2000000000 | bytes 2000000 | tf_op jit(solution)/shard_map/pallas_call | solution.py:641
  50.7 0.0 copy-done
  50.7 0.0 copy-done.1
  50.7 1.2 %shard_map.77 = (bf16[32,2,16,128]{3,2,1,0:T(8,128)(2,1)}, f32[9,96,32]{2,1,0:T(8,128)}, f32[9,96,32]{2,1,0:T(8,128)}) custom-call(f32[16,2,2,8,128]{4,3,2,1,0:T(8,128)S(1)} %get-tuple-element.8.tot, bf16[32,2,16,128]{3,2,1,0:T(8,128)(2,1)S(1)} %get-tuple-element.9.jv_in, bf16[864,32]{1,0:T(8,128)(2,1)S(1)} %bitcast.7, bf16[864,32]{1,0:T(8,128)(2,1)S(1)} %bitcast.9), custom_call_target="tpu_custom_call" | custom-call | tf_op jit(solution)/shard_map/pallas_call | solution.py:686
Async XLA Ops:
  0.6 50.0 %copy-start = (bf16[3,3,3,32,32]{4,3,2,1,0:T(8,128)(2,1)S(1)}, bf16[3,3,3,32,32]{4,3,2,1,0:T(8,128)(2,1)}, u32[]{:S(2)}) copy-start(bf16[3,3,3,32,32]{4,3,2,1,0:T(8,128)(2,1)} %param.8) | copy-start | bytes 165892
  0.6 50.0 %copy-start.1 = (bf16[3,3,3,32,32]{4,3,2,1,0:T(8,128)(2,1)S(1)}, bf16[3,3,3,32,32]{4,3,2,1,0:T(8,128)(2,1)}, u32[]{:S(2)}) copy-start(bf16[3,3,3,32,32]{4,3,2,1,0:T(8,128)(2,1)} %param.9) | copy-start | bytes 165892
